TPU v7x, 128 devices: a whole 4x4x4 slice. The times are simulated.
128 devices in a mesh: tp: 2 (over core), fsdp: 64 (over z, y, x).
Axes of the slice: x: 4, y: 4, z: 4, core: 2. Of those that a mesh axis runs over, the one named last changes fastest.
Arguments:
- emb_table: float32 [16384, 1152], P('tp', 'fsdp')
- tok_ids: int32 [64, 1024], P('fsdp')
- lab_ids: int32 [64, 1024], P('fsdp')
- h_last: bfloat16 [64, 1024, 1152], P('fsdp')
- g_embed: bfloat16 [64, 1024, 1152], P('fsdp')
- norm_w: float32 [1152], P('fsdp')
Outputs:
- output 1: bfloat16 [64, 1024, 1152], P('fsdp')
- output 2: float32 [], replicated
- output 3: bfloat16 [64, 1024, 1152], P('fsdp')
- output 4: float32 [1152], P('fsdp')
- output 5: float32 [16384, 1152], P('tp', 'fsdp')
All inputs are finite; a program needn't handle non-finite values.
Results may differ from a plain program's by a relative error of at most 0.001.
Values are sent between devices in bfloat16 or wider.
A program may use at most 1 GiB of HBM per device.

v0:
```python
import math
import jax
import jax.numpy as jnp
from jax import lax
from jax.sharding import PartitionSpec as P

SOFT_CAP = 30.0
NORM_EPS = 1e-6


def solution(mesh):
    fsdp_size = mesh.shape["fsdp"]

    def device_step(emb_shard, tok_ids, lab_ids, h_last, g_embed, norm_w):
        vocab_rows = emb_shard.shape[0]
        batch_loc, seq_len, width = h_last.shape
        tok_count = batch_loc * seq_len
        total_tokens = tok_count * fsdp_size
        row_start = lax.axis_index("tp") * vocab_rows
        vocab_iota = jnp.arange(vocab_rows, dtype=jnp.int32)
        emb_scale = jnp.asarray(math.sqrt(width), jnp.bfloat16).astype(jnp.float32)
        shard_bf = emb_shard.astype(jnp.bfloat16)

        table_look = lax.all_gather(shard_bf, "fsdp", axis=1, tiled=True)
        tok_local = tok_ids.reshape(tok_count) - row_start
        in_block = (tok_local >= 0) & (tok_local < vocab_rows)
        row_vals = jnp.take(table_look, jnp.clip(tok_local, 0, vocab_rows - 1), axis=0)
        row_vals = lax.psum(jnp.where(in_block[:, None], row_vals, jnp.zeros_like(row_vals)), "tp")
        x_emb = (row_vals.astype(jnp.float32) * emb_scale).astype(jnp.bfloat16)

        norm_gain = 1.0 + lax.all_gather(norm_w, "fsdp", axis=0, tiled=True)
        h_wide = h_last.reshape(tok_count, width).astype(jnp.float32)
        inv_rms = lax.rsqrt(jnp.mean(h_wide * h_wide, axis=1, keepdims=True) + NORM_EPS)
        h_norm = h_wide * inv_rms
        x_norm = (h_norm * norm_gain).astype(jnp.bfloat16)

        table_head = lax.all_gather(shard_bf, "fsdp", axis=1, tiled=True)
        logits = jnp.einsum("td,vd->tv", x_norm, table_head, preferred_element_type=jnp.float32)
        tanh_z = jnp.tanh(logits / SOFT_CAP)
        capped = SOFT_CAP * tanh_z
        exp_shift = jnp.exp(capped - SOFT_CAP)
        lab_hit = (lab_ids.reshape(tok_count) - row_start)[:, None] == vocab_iota[None, :]
        tok_stats = jnp.stack([jnp.sum(exp_shift, axis=1), jnp.sum(jnp.where(lab_hit, capped, 0.0), axis=1)])
        tok_stats = lax.psum(tok_stats, "tp")
        sum_exp = tok_stats[0]
        log_norm = jnp.log(sum_exp) + SOFT_CAP
        loss_val = lax.psum(jnp.sum(log_norm - tok_stats[1]), "fsdp") / total_tokens

        soft_prob = exp_shift / sum_exp[:, None]
        d_logits = ((soft_prob - lab_hit.astype(jnp.float32)) * (1.0 - tanh_z * tanh_z) / total_tokens).astype(jnp.bfloat16)
        d_xnorm = lax.psum(jnp.dot(d_logits, table_head, preferred_element_type=jnp.float32), "tp")
        g_dir = d_xnorm * norm_gain
        d_hidden = (inv_rms * (g_dir - h_norm * jnp.mean(g_dir * h_norm, axis=1, keepdims=True))).astype(jnp.bfloat16)
        d_norm_w = lax.psum_scatter(jnp.sum(d_xnorm * h_norm, axis=0), "fsdp", scatter_dimension=0, tiled=True)

        head_part = jnp.einsum("tv,td->vd", d_logits, x_norm, preferred_element_type=jnp.float32)
        d_head = lax.psum_scatter(head_part, "fsdp", scatter_dimension=1, tiled=True)
        tok_hit = (tok_local[:, None] == vocab_iota[None, :]).astype(jnp.bfloat16)
        look_part = jnp.einsum("tv,td->vd", tok_hit, g_embed.reshape(tok_count, width), preferred_element_type=jnp.float32)
        d_look = lax.psum_scatter(look_part, "fsdp", scatter_dimension=1, tiled=True)
        d_table = d_head + emb_scale * d_look
        return (x_emb.reshape(batch_loc, seq_len, width), loss_val, d_hidden.reshape(batch_loc, seq_len, width), d_norm_w, d_table)

    spec_tok = P("fsdp", None)
    spec_act = P("fsdp", None, None)
    return jax.shard_map(device_step, mesh=mesh, in_specs=(P("tp", "fsdp"), spec_tok, spec_tok, spec_act, spec_act, P("fsdp")), out_specs=(spec_act, P(), spec_act, P("fsdp"), P("tp", "fsdp")), check_vma=False)
```

profile of v0, /device:TPU:0, one launch (start us, length us, event | category | flops | bytes accessed | tf_op | source)
XLA Modules:
  0.0 2343.2 jit_solution(3881444960182220895)
XLA Ops:
  7.2 2.1 convert_bitcast_fusion
  9.4 0.7 compare_select_fusion
  10.1 25.7 %fusion.2 = f32[8192,1152]{0,1:T(8,128)} fusion(s32[1024]{0:T(1024)S(1)} %bitcast.46, bf16[1,1024,1152]{2,1,0:T(8,128)(2,1)S(1)} %copy-done), kind=kOutput, calls=%fused_computation.7 | convolution fusion | flops 19335741440 | bytes 40112128 | tf_op jit(solution)/shard_map/tv,td->vd/dot_general | solution.py:59
  35.8 575.1 %fusion.1 = f32[8192,24]{0,1:T(8,128)S(1)} fusion(f32[8192,1152]{0,1:T(8,128)} %fusion.2), kind=kCustom, calls=%all-reduce-scatter.1 | all-reduce-scatter fusion | flops 12582913 | bytes 38535680
  610.9 2.2 collective-permute-start.30
  613.1 3.6 collective-permute-start.29
  616.7 4.9 collective-permute-start.28
  621.6 4.3 collective-permute-start.27
  625.9 0.9 slice.13
  626.8 3.0 collective-permute-start.31
  629.8 0.6 fusion.25
  631.4 235.5 %all-reduce = f32[1152]{0:T(1024)S(1)} all-reduce(f32[1152]{0:T(1024)S(1)} %dynamic-update-slice), channel_id=1, replica_groups=mesh['tp'=2,'fsdp'=64] {'fsdp'}, use_global_device_ids=true, to_apply=%add | all-reduce | flops 1152 | bytes 9216
  867.0 0.5 fusion.15
  867.6 22.3 reshape.105
  889.8 24.6 %copy.13 = bf16[1152,8192]{0,1:T(8,128)(2,1)} copy(bf16[1152,8192]{1,0:T(8,128)(2,1)} %reshape.105) | data formatting | bytes 37748736
  914.4 15.1 gather_fusion
  929.6 3.2 select_select_fusion
  932.8 0.3 all-reduce.12.cloned.1.call-start
  933.1 36.3 %fusion.3 = (f32[1024]{0:T(1024)S(1)}, f32[1024]{0:T(1024)S(1)}, f32[1024,8192]{1,0:T(8,128)}) fusion(s32[1024]{0:T(1024)S(1)} %bitcast.49, bf16[1152,8192]{1,0:T(8,128)(2,1)} %reshape.105, bf16[1,1024,1152]{2,1,0:T(8,128)(2,1)S(1)} %copy-done.2, f32[1152]{0:T(1024)S(1)} %broadcast_add_fusion, f32[1024]{0:T(1024)S(1)} %add_rsqrt_fusion), kind=kOutput, calls=%fused_computation.8 | convolution fusion | flops 19390791680 | bytes 54809088 | tf_op jit(solution)/shard_map/td,vd->tv/dot_general | solution.py:38
  969.3 3.0 psum.29
  972.3 19.4 multiply_convert_fusion
  991.7 2.7 collective-permute-start.26
  994.5 3.3 copy-done.3
  997.8 25.8 %fusion.26 = f32[1024,1152]{1,0:T(8,128)} fusion(bf16[1024,8192]{1,0:T(8,128)(2,1)S(1)} %multiply_convert_fusion, bf16[1152,8192]{1,0:T(8,128)(2,1)} %reshape.105), kind=kOutput, calls=%fused_computation.47 | convolution fusion | flops 19327352832 | bytes 40370176 | tf_op jit(solution)/shard_map/dot_general | solution.py:51
  1023.5 2.2 collective-permute-start.25
  1025.7 2.2 collective-permute-start.24
  1028.0 2.2 collective-permute-start.23
  1030.2 2.2 collective-permute-start.22
  1032.4 2.3 collective-permute-start.21
  1034.7 28.1 %fusion.20 = f32[8192,1152]{0,1:T(8,128)} fusion(bf16[1024,8192]{1,0:T(8,128)(2,1)} %copy-done.3, bf16[1,1024,1152]{2,1,0:T(8,128)(2,1)S(1)} %copy-done.2, f32[1152]{0:T(1024)S(1)} %broadcast_add_fusion, f32[1024]{0:T(1024)S(1)} %add_rsqrt_fusion), kind=kOutput, calls=%fused_computation.30 | convolution fusion | flops 19332071424 | bytes 56893952 | tf_op jit(solution)/shard_map/tv,td->vd/dot_general | solution.py:56
  1062.9 1.3 collective-permute-start.20
  1064.2 4.9 collective-permute-done.24
  1069.2 24.3 %collective-permute-start.19 = (f32[8192,24]{0,1:T(8,128)S(1)}, f32[8192,24]{0,1:T(8,128)S(1)}, u32[]{:S(2)}, u32[]{:S(2)}) collective-permute-start(f32[8192,24]{0,1:T(8,128)S(1)} %fusion.1), channel_id=1, source_target_pairs={{0,4},{1,5},{2,6},{3,7},{4,8},{5,9},{6,10},{7,11},{8,12},{9,13},{1... | collective-permute-start | bytes 2359304
  1093.5 29.7 %collective-permute-start.18 = (f32[8192,24]{0,1:T(8,128)S(1)}, f32[8192,24]{0,1:T(8,128)}, u32[]{:S(2)}, u32[]{:S(2)}) collective-permute-start(f32[8192,24]{0,1:T(8,128)S(1)} %fusion.1), channel_id=1, source_target_pairs={{0,3},{1,4},{2,5},{3,6},{4,7},{5,8},{6,9},{7,10},{8,11},{9,12},{10... | collective-permute-start | bytes 2359304
  1123.2 9.9 collective-permute-start.17
  1133.1 2.2 collective-permute-start.16
  1135.3 580.9 %fusion = f32[8192,24]{0,1:T(8,128)S(1)} fusion(f32[8192,1152]{0,1:T(8,128)} %fusion.20), kind=kCustom, calls=%all-reduce-scatter | all-reduce-scatter fusion | flops 12582913 | bytes 38535680
  1716.3 5.2 collective-permute-start.15
  1721.5 1.3 collective-permute-start.14
  1722.8 1.3 collective-permute-start.13
  1724.2 19.9 collective-permute-start.12
  1744.1 24.0 %collective-permute-start.11 = (f32[8192,24]{0,1:T(8,128)S(1)}, f32[8192,24]{0,1:T(8,128)S(1)}, u32[]{:S(2)}, u32[]{:S(2)}) collective-permute-start(f32[8192,24]{0,1:T(8,128)S(1)} %fusion), channel_id=1, source_target_pairs={{0,12},{1,13},{2,14},{3,15},{4,16},{5,17},{6,18},{7,19},{8,20},{9,... | collective-permute-start | bytes 2359304
  1768.2 34.6 %collective-permute-done.15 = f32[8192,18]{0,1:T(8,128)S(1)} collective-permute-done((f32[8192,18]{0,1:T(8,128)S(1)}, f32[8192,18]{0,1:T(8,128)S(1)}, u32[]{:S(2)}, u32[]{:S(2)}) %collective-permute-start.15) | collective-permute-done | bytes 589856
  1802.7 12.0 collective-permute-start.10
  1814.8 9.7 collective-permute-start.9
  1824.6 1.3 collective-permute-start.8
  1825.9 25.4 %collective-permute-start.7 = (f32[8192,24]{0,1:T(8,128)S(1)}, f32[8192,24]{0,1:T(8,128)S(1)}, u32[]{:S(2)}, u32[]{:S(2)}) collective-permute-start(f32[8192,24]{0,1:T(8,128)S(1)} %fusion), channel_id=1, source_target_pairs={{0,8},{1,9},{2,10},{3,11},{4,12},{5,13},{6,14},{7,15},{8,16},{9,17... | collective-permute-start | bytes 2359304
  1851.4 1.3 collective-permute-start.6
  1852.8 1.3 collective-permute-start.5
  1854.2 32.7 %collective-permute-start.4 = (f32[8192,24]{0,1:T(8,128)S(1)}, f32[8192,24]{0,1:T(8,128)}, u32[]{:S(2)}, u32[]{:S(2)}) collective-permute-start(f32[8192,24]{0,1:T(8,128)S(1)} %fusion), channel_id=1, source_target_pairs={{0,5},{1,6},{2,7},{3,8},{4,9},{5,10},{6,11},{7,12},{8,13},{9,14},{... | collective-permute-start | bytes 2359304
  1886.9 10.0 collective-permute-start.3
  1896.8 21.6 collective-permute-done.7
  1918.4 23.1 collective-permute-start.2
  1941.5 2.2 collective-permute-start.1
  1943.7 7.6 collective-permute-start
  1952.8 87.5 %concatenate.1 = f32[8192,402]{0,1:T(8,128)} concatenate(f32[8192,18]{0,1:T(8,128)} %collective-permute-done.31, f32[8192,24]{0,1:T(8,128)} %collective-permute-done.30, f32[8192,24]{0,1:T(8,128)} %collective-permute-done.29, f32[8192,24]{0,1:T(8,128)} %collective-permute-done.28, f32[8192,24]{0,1:T(8,128)} %collective-permute-done.27, f32[8192,24]{0,1:T(8,128)} %collective-permute-done.26, ...), dimensions={1} | concatenate | bytes 26345472
  2040.2 0.6 subtract_reduce_fusion
  2040.9 88.5 %concatenate = f32[8192,402]{0,1:T(8,128)} concatenate(f32[8192,18]{0,1:T(8,128)} %copy-done.4, f32[8192,24]{0,1:T(8,128)} %copy-done.5, f32[8192,24]{0,1:T(8,128)} %copy-done.6, f32[8192,24]{0,1:T(8,128)} %copy-done.7, f32[8192,24]{0,1:T(8,128)} %copy-done.8, f32[8192,24]{0,1:T(8,128)} %copy-done.9, f32[8192,24]{0,1:T(8,128)} %copy-done.10, f32[8192,24]{0,1:T(8,128)} %copy-done.11, ...), dimensions={1} | concatenate | bytes 26345472
  2129.3 2.6 fusion.19
  2131.9 3.6 fusion.16
  2135.6 4.3 fusion.14
  2139.9 189.5 %all-reduce.6 = (f32[]{:T(128)}, f32[1152]{0:T(1024)S(1)}) all-reduce(f32[]{:T(128)} %subtract_reduce_fusion, f32[1152]{0:T(1024)S(1)} %get-tuple-element.7), channel_id=1, replica_groups=mesh['tp'=2,'fsdp'=64] {'fsdp'}, use_global_device_ids=true, to_apply=%region_6.7 | all-reduce | flops 1153 | bytes 9224 | tf_op jit(solution)/shard_map/psum | solution.py:47
  2330.1 0.6 dynamic-slice.2
  2330.7 4.6 fusion.17
  (83 shorter events, 0.7 us)
Async XLA Ops:
  7.2 2.9 copy-start
  7.2 860.4 %all-gather.3.cloned.1.call-start = ((), (), s32[]{:S(2)}) async-start(), calls=%async_computation.2 | async-start | bytes 25559040 | tf_op jit(solution)/shard_map/all_gather | solution.py:24
  9.3 2122.6 %all-reduce.10.cloned.1.call-start = ((), (), s32[]{:S(2)}) async-start(), calls=%async_computation | async-start | bytes 4718592 | tf_op jit(solution)/shard_map/psum | solution.py:28
  35.8 594.1 %copy-start.15 = (u32[128]{0:T(128)S(1)}, u32[128]{0:T(128)}, u32[]{:S(2)}) copy-start(u32[128]{0:T(128)} %constant.63) | copy-start | bytes 1540
  35.8 595.3 %copy-start.17 = (f32[18]{0:T(128)S(1)}, f32[18]{0:T(128)}, u32[]{:S(2)}) copy-start(f32[18]{0:T(128)} %param.11) | copy-start | bytes 220
  35.8 831.2 %copy-start.16 = (s32[1,1024]{1,0:T(1,128)S(1)}, s32[1,1024]{1,0:T(1,128)}, u32[]{:S(2)}) copy-start(s32[1,1024]{1,0:T(1,128)} %param.8) | copy-start | bytes 12292
  35.8 831.2 %copy-start.2 = (bf16[1,1024,1152]{2,1,0:T(8,128)(2,1)S(1)}, bf16[1,1024,1152]{2,1,0:T(8,128)(2,1)}, u32[]{:S(2)}) copy-start(bf16[1,1024,1152]{2,1,0:T(8,128)(2,1)} %param.9) | copy-start | bytes 7077892
  610.9 412.7 %collective-permute-start.30 = (f32[8192,24]{0,1:T(8,128)S(1)}, f32[8192,24]{0,1:T(8,128)}, u32[]{:S(2)}, u32[]{:S(2)}) collective-permute-start(f32[8192,24]{0,1:T(8,128)S(1)} %fusion.1), channel_id=1, source_target_pairs={{0,15},{1,16},{2,17},{3,18},{4,19},{5,20},{6,21},{7,22},{8,23},{9,... | collective-permute-start | bytes 2359304
  613.1 412.7 %collective-permute-start.29 = (f32[8192,24]{0,1:T(8,128)S(1)}, f32[8192,24]{0,1:T(8,128)}, u32[]{:S(2)}, u32[]{:S(2)}) collective-permute-start(f32[8192,24]{0,1:T(8,128)S(1)} %fusion.1), channel_id=1, source_target_pairs={{0,14},{1,15},{2,16},{3,17},{4,18},{5,19},{6,20},{7,21},{8,22},{9,... | collective-permute-start | bytes 2359304
  616.7 411.2 %collective-permute-start.28 = (f32[8192,24]{0,1:T(8,128)S(1)}, f32[8192,24]{0,1:T(8,128)}, u32[]{:S(2)}, u32[]{:S(2)}) collective-permute-start(f32[8192,24]{0,1:T(8,128)S(1)} %fusion.1), channel_id=1, source_target_pairs={{0,13},{1,14},{2,15},{3,16},{4,17},{5,18},{6,19},{7,20},{8,21},{9,... | collective-permute-start | bytes 2359304
  621.6 408.6 %collective-permute-start.27 = (f32[8192,24]{0,1:T(8,128)S(1)}, f32[8192,24]{0,1:T(8,128)}, u32[]{:S(2)}, u32[]{:S(2)}) collective-permute-start(f32[8192,24]{0,1:T(8,128)S(1)} %fusion.1), channel_id=1, source_target_pairs={{0,12},{1,13},{2,14},{3,15},{4,16},{5,17},{6,18},{7,19},{8,20},{9,... | collective-permute-start | bytes 2359304
  626.8 364.9 %collective-permute-start.31 = (f32[8192,18]{0,1:T(8,128)}, f32[8192,18]{0,1:T(8,128)}, u32[]{:S(2)}, u32[]{:S(2)}) collective-permute-start(f32[8192,18]{0,1:T(8,128)} %slice.13), channel_id=1, source_target_pairs={{0,16},{1,17},{2,18},{3,19},{4,20},{5,21},{6,22},{7,23},{8,24},{9,... | collective-permute-start | bytes 1769480
  932.8 1202.8 %all-reduce.12.cloned.1.call-start = ((), (), s32[]{:S(2)}) async-start(), calls=%async_computation.1 | async-start | bytes 9437184 | tf_op jit(solution)/shard_map/psum | solution.py:51
  991.7 6.1 copy-start.3
  991.7 40.6 %collective-permute-start.26 = (f32[8192,24]{0,1:T(8,128)S(1)}, f32[8192,24]{0,1:T(8,128)}, u32[]{:S(2)}, u32[]{:S(2)}) collective-permute-start(f32[8192,24]{0,1:T(8,128)S(1)} %fusion.1), channel_id=1, source_target_pairs={{0,11},{1,12},{2,13},{3,14},{4,15},{5,16},{6,17},{7,18},{8,19},{9,... | collective-permute-start | bytes 2359304
  1023.5 39.3 %collective-permute-start.25 = (f32[8192,24]{0,1:T(8,128)S(1)}, f32[8192,24]{0,1:T(8,128)}, u32[]{:S(2)}, u32[]{:S(2)}) collective-permute-start(f32[8192,24]{0,1:T(8,128)S(1)} %fusion.1), channel_id=1, source_target_pairs={{0,10},{1,11},{2,12},{3,13},{4,14},{5,15},{6,16},{7,17},{8,18},{9,... | collective-permute-start | bytes 2359304
  1025.7 43.4 %collective-permute-start.24 = (f32[8192,24]{0,1:T(8,128)S(1)}, f32[8192,24]{0,1:T(8,128)}, u32[]{:S(2)}, u32[]{:S(2)}) collective-permute-start(f32[8192,24]{0,1:T(8,128)S(1)} %fusion.1), channel_id=1, source_target_pairs={{0,9},{1,10},{2,11},{3,12},{4,13},{5,14},{6,15},{7,16},{8,17},{9,1... | collective-permute-start | bytes 2359304
  1028.0 65.5 %collective-permute-start.23 = (f32[8192,24]{0,1:T(8,128)S(1)}, f32[8192,24]{0,1:T(8,128)}, u32[]{:S(2)}, u32[]{:S(2)}) collective-permute-start(f32[8192,24]{0,1:T(8,128)S(1)} %fusion.1), channel_id=1, source_target_pairs={{0,8},{1,9},{2,10},{3,11},{4,12},{5,13},{6,14},{7,15},{8,16},{9,17... | collective-permute-start | bytes 2359304
  1030.2 93.1 %collective-permute-start.22 = (f32[8192,24]{0,1:T(8,128)S(1)}, f32[8192,24]{0,1:T(8,128)}, u32[]{:S(2)}, u32[]{:S(2)}) collective-permute-start(f32[8192,24]{0,1:T(8,128)S(1)} %fusion.1), channel_id=1, source_target_pairs={{0,7},{1,8},{2,9},{3,10},{4,11},{5,12},{6,13},{7,14},{8,15},{9,16}... | collective-permute-start | bytes 2359304
  1032.4 100.8 %collective-permute-start.21 = (f32[8192,24]{0,1:T(8,128)S(1)}, f32[8192,24]{0,1:T(8,128)}, u32[]{:S(2)}, u32[]{:S(2)}) collective-permute-start(f32[8192,24]{0,1:T(8,128)S(1)} %fusion.1), channel_id=1, source_target_pairs={{0,6},{1,7},{2,8},{3,9},{4,10},{5,11},{6,12},{7,13},{8,14},{9,15},... | collective-permute-start | bytes 2359304
  1062.9 653.4 %collective-permute-start.20 = (f32[8192,24]{0,1:T(8,128)S(1)}, f32[8192,24]{0,1:T(8,128)S(1)}, u32[]{:S(2)}, u32[]{:S(2)}) collective-permute-start(f32[8192,24]{0,1:T(8,128)S(1)} %fusion.1), channel_id=1, source_target_pairs={{0,5},{1,6},{2,7},{3,8},{4,9},{5,10},{6,11},{7,12},{8,13},{9,14},{... | collective-permute-start | bytes 2359304
  1069.2 652.3 %collective-permute-start.19 = (f32[8192,24]{0,1:T(8,128)S(1)}, f32[8192,24]{0,1:T(8,128)S(1)}, u32[]{:S(2)}, u32[]{:S(2)}) collective-permute-start(f32[8192,24]{0,1:T(8,128)S(1)} %fusion.1), channel_id=1, source_target_pairs={{0,4},{1,5},{2,6},{3,7},{4,8},{5,9},{6,10},{7,11},{8,12},{9,13},{1... | collective-permute-start | bytes 2359304
  1093.5 629.4 %collective-permute-start.18 = (f32[8192,24]{0,1:T(8,128)S(1)}, f32[8192,24]{0,1:T(8,128)}, u32[]{:S(2)}, u32[]{:S(2)}) collective-permute-start(f32[8192,24]{0,1:T(8,128)S(1)} %fusion.1), channel_id=1, source_target_pairs={{0,3},{1,4},{2,5},{3,6},{4,7},{5,8},{6,9},{7,10},{8,11},{9,12},{10... | collective-permute-start | bytes 2359304
  1123.2 601.0 %collective-permute-start.17 = (f32[8192,24]{0,1:T(8,128)S(1)}, f32[8192,24]{0,1:T(8,128)}, u32[]{:S(2)}, u32[]{:S(2)}) collective-permute-start(f32[8192,24]{0,1:T(8,128)S(1)} %fusion.1), channel_id=1, source_target_pairs={{0,2},{1,3},{2,4},{3,5},{4,6},{5,7},{6,8},{7,9},{8,10},{9,11},{10,... | collective-permute-start | bytes 2359304
  1133.1 611.0 %collective-permute-start.16 = (f32[8192,24]{0,1:T(8,128)S(1)}, f32[8192,24]{0,1:T(8,128)}, u32[]{:S(2)}, u32[]{:S(2)}) collective-permute-start(f32[8192,24]{0,1:T(8,128)S(1)} %fusion.1), channel_id=1, source_target_pairs={{0,1},{1,2},{2,3},{3,4},{4,5},{5,6},{6,7},{7,8},{8,9},{9,10},{10,1... | collective-permute-start | bytes 2359304
  1716.3 86.5 %collective-permute-start.15 = (f32[8192,18]{0,1:T(8,128)S(1)}, f32[8192,18]{0,1:T(8,128)S(1)}, u32[]{:S(2)}, u32[]{:S(2)}) collective-permute-start(f32[8192,18]{0,1:T(8,128)S(1)} %slice.12), channel_id=1, source_target_pairs={{0,16},{1,17},{2,18},{3,19},{4,20},{5,21},{6,22},{7,23},{8,24},{9,... | collective-permute-start | bytes 1769480
  1721.5 93.3 %collective-permute-start.14 = (f32[8192,24]{0,1:T(8,128)S(1)}, f32[8192,24]{0,1:T(8,128)S(1)}, u32[]{:S(2)}, u32[]{:S(2)}) collective-permute-start(f32[8192,24]{0,1:T(8,128)S(1)} %fusion), channel_id=1, source_target_pairs={{0,15},{1,16},{2,17},{3,18},{4,19},{5,20},{6,21},{7,22},{8,23},{9,... | collective-permute-start | bytes 2359304
  1722.8 101.7 %collective-permute-start.13 = (f32[8192,24]{0,1:T(8,128)S(1)}, f32[8192,24]{0,1:T(8,128)S(1)}, u32[]{:S(2)}, u32[]{:S(2)}) collective-permute-start(f32[8192,24]{0,1:T(8,128)S(1)} %fusion), channel_id=1, source_target_pairs={{0,14},{1,15},{2,16},{3,17},{4,18},{5,19},{6,20},{7,21},{8,22},{9,... | collective-permute-start | bytes 2359304
  1724.2 101.7 %collective-permute-start.12 = (f32[8192,24]{0,1:T(8,128)S(1)}, f32[8192,24]{0,1:T(8,128)S(1)}, u32[]{:S(2)}, u32[]{:S(2)}) collective-permute-start(f32[8192,24]{0,1:T(8,128)S(1)} %fusion), channel_id=1, source_target_pairs={{0,13},{1,14},{2,15},{3,16},{4,17},{5,18},{6,19},{7,20},{8,21},{9,... | collective-permute-start | bytes 2359304
  1744.1 107.3 %collective-permute-start.11 = (f32[8192,24]{0,1:T(8,128)S(1)}, f32[8192,24]{0,1:T(8,128)S(1)}, u32[]{:S(2)}, u32[]{:S(2)}) collective-permute-start(f32[8192,24]{0,1:T(8,128)S(1)} %fusion), channel_id=1, source_target_pairs={{0,12},{1,13},{2,14},{3,15},{4,16},{5,17},{6,18},{7,19},{8,20},{9,... | collective-permute-start | bytes 2359304
  1802.7 141.0 %copy-start.4 = (f32[8192,18]{0,1:T(8,128)}, f32[8192,18]{0,1:T(8,128)S(1)}, u32[]{:S(2)}) copy-start(f32[8192,18]{0,1:T(8,128)S(1)} %collective-permute-done.15) | copy-start | bytes 1769476
  1802.7 50.0 %collective-permute-start.10 = (f32[8192,24]{0,1:T(8,128)S(1)}, f32[8192,24]{0,1:T(8,128)S(1)}, u32[]{:S(2)}, u32[]{:S(2)}) collective-permute-start(f32[8192,24]{0,1:T(8,128)S(1)} %fusion), channel_id=1, source_target_pairs={{0,11},{1,12},{2,13},{3,14},{4,15},{5,16},{6,17},{7,18},{8,19},{9,... | collective-permute-start | bytes 2359304
  1814.8 136.6 %copy-start.5 = (f32[8192,24]{0,1:T(8,128)}, f32[8192,24]{0,1:T(8,128)S(1)}, u32[]{:S(2)}) copy-start(f32[8192,24]{0,1:T(8,128)S(1)} %collective-permute-done.14) | copy-start | bytes 2359300
  1814.8 39.3 %collective-permute-start.9 = (f32[8192,24]{0,1:T(8,128)S(1)}, f32[8192,24]{0,1:T(8,128)S(1)}, u32[]{:S(2)}, u32[]{:S(2)}) collective-permute-start(f32[8192,24]{0,1:T(8,128)S(1)} %fusion), channel_id=1, source_target_pairs={{0,10},{1,11},{2,12},{3,13},{4,14},{5,15},{6,16},{7,17},{8,18},{9,... | collective-permute-start | bytes 2359304
  1824.6 126.8 %copy-start.6 = (f32[8192,24]{0,1:T(8,128)}, f32[8192,24]{0,1:T(8,128)S(1)}, u32[]{:S(2)}) copy-start(f32[8192,24]{0,1:T(8,128)S(1)} %collective-permute-done.13) | copy-start | bytes 2359300
  1824.6 62.3 %collective-permute-start.8 = (f32[8192,24]{0,1:T(8,128)S(1)}, f32[8192,24]{0,1:T(8,128)S(1)}, u32[]{:S(2)}, u32[]{:S(2)}) collective-permute-start(f32[8192,24]{0,1:T(8,128)S(1)} %fusion), channel_id=1, source_target_pairs={{0,9},{1,10},{2,11},{3,12},{4,13},{5,14},{6,15},{7,16},{8,17},{9,1... | collective-permute-start | bytes 2359304
  1825.9 125.5 %copy-start.7 = (f32[8192,24]{0,1:T(8,128)}, f32[8192,24]{0,1:T(8,128)S(1)}, u32[]{:S(2)}) copy-start(f32[8192,24]{0,1:T(8,128)S(1)} %collective-permute-done.12) | copy-start | bytes 2359300
  1825.9 92.5 %collective-permute-start.7 = (f32[8192,24]{0,1:T(8,128)S(1)}, f32[8192,24]{0,1:T(8,128)S(1)}, u32[]{:S(2)}, u32[]{:S(2)}) collective-permute-start(f32[8192,24]{0,1:T(8,128)S(1)} %fusion), channel_id=1, source_target_pairs={{0,8},{1,9},{2,10},{3,11},{4,12},{5,13},{6,14},{7,15},{8,16},{9,17... | collective-permute-start | bytes 2359304
  1851.4 100.0 %copy-start.8 = (f32[8192,24]{0,1:T(8,128)}, f32[8192,24]{0,1:T(8,128)S(1)}, u32[]{:S(2)}) copy-start(f32[8192,24]{0,1:T(8,128)S(1)} %collective-permute-done.11) | copy-start | bytes 2359300
  1851.4 90.1 %collective-permute-start.6 = (f32[8192,24]{0,1:T(8,128)S(1)}, f32[8192,24]{0,1:T(8,128)S(1)}, u32[]{:S(2)}, u32[]{:S(2)}) collective-permute-start(f32[8192,24]{0,1:T(8,128)S(1)} %fusion), channel_id=1, source_target_pairs={{0,7},{1,8},{2,9},{3,10},{4,11},{5,12},{6,13},{7,14},{8,15},{9,16}... | collective-permute-start | bytes 2359304
  1852.8 98.6 %copy-start.9 = (f32[8192,24]{0,1:T(8,128)}, f32[8192,24]{0,1:T(8,128)S(1)}, u32[]{:S(2)}) copy-start(f32[8192,24]{0,1:T(8,128)S(1)} %collective-permute-done.10) | copy-start | bytes 2359300
  1852.8 90.9 %collective-permute-start.5 = (f32[8192,24]{0,1:T(8,128)S(1)}, f32[8192,24]{0,1:T(8,128)S(1)}, u32[]{:S(2)}, u32[]{:S(2)}) collective-permute-start(f32[8192,24]{0,1:T(8,128)S(1)} %fusion), channel_id=1, source_target_pairs={{0,6},{1,7},{2,8},{3,9},{4,10},{5,11},{6,12},{7,13},{8,14},{9,15},... | collective-permute-start | bytes 2359304
  1854.1 97.3 %copy-start.10 = (f32[8192,24]{0,1:T(8,128)}, f32[8192,24]{0,1:T(8,128)S(1)}, u32[]{:S(2)}) copy-start(f32[8192,24]{0,1:T(8,128)S(1)} %collective-permute-done.9) | copy-start | bytes 2359300
  1854.2 186.7 %collective-permute-start.4 = (f32[8192,24]{0,1:T(8,128)S(1)}, f32[8192,24]{0,1:T(8,128)}, u32[]{:S(2)}, u32[]{:S(2)}) collective-permute-start(f32[8192,24]{0,1:T(8,128)S(1)} %fusion), channel_id=1, source_target_pairs={{0,5},{1,6},{2,7},{3,8},{4,9},{5,10},{6,11},{7,12},{8,13},{9,14},{... | collective-permute-start | bytes 2359304
  1886.9 64.6 %copy-start.11 = (f32[8192,24]{0,1:T(8,128)}, f32[8192,24]{0,1:T(8,128)S(1)}, u32[]{:S(2)}) copy-start(f32[8192,24]{0,1:T(8,128)S(1)} %collective-permute-done.8) | copy-start | bytes 2359300
  1886.9 154.0 %collective-permute-start.3 = (f32[8192,24]{0,1:T(8,128)S(1)}, f32[8192,24]{0,1:T(8,128)}, u32[]{:S(2)}, u32[]{:S(2)}) collective-permute-start(f32[8192,24]{0,1:T(8,128)S(1)} %fusion), channel_id=1, source_target_pairs={{0,4},{1,5},{2,6},{3,7},{4,8},{5,9},{6,10},{7,11},{8,12},{9,13},{1... | collective-permute-start | bytes 2359304
  1918.4 33.0 %copy-start.12 = (f32[8192,24]{0,1:T(8,128)}, f32[8192,24]{0,1:T(8,128)S(1)}, u32[]{:S(2)}) copy-start(f32[8192,24]{0,1:T(8,128)S(1)} %collective-permute-done.7) | copy-start | bytes 2359300
  1918.4 122.4 %collective-permute-start.2 = (f32[8192,24]{0,1:T(8,128)S(1)}, f32[8192,24]{0,1:T(8,128)}, u32[]{:S(2)}, u32[]{:S(2)}) collective-permute-start(f32[8192,24]{0,1:T(8,128)S(1)} %fusion), channel_id=1, source_target_pairs={{0,3},{1,4},{2,5},{3,6},{4,7},{5,8},{6,9},{7,10},{8,11},{9,12},{10... | collective-permute-start | bytes 2359304
  1941.5 9.9 copy-start.13
  1941.5 99.3 %collective-permute-start.1 = (f32[8192,24]{0,1:T(8,128)S(1)}, f32[8192,24]{0,1:T(8,128)}, u32[]{:S(2)}, u32[]{:S(2)}) collective-permute-start(f32[8192,24]{0,1:T(8,128)S(1)} %fusion), channel_id=1, source_target_pairs={{0,2},{1,3},{2,4},{3,5},{4,6},{5,7},{6,8},{7,9},{8,10},{9,11},{10,... | collective-permute-start | bytes 2359304
  1943.7 7.7 copy-start.14
  1943.7 97.1 %collective-permute-start = (f32[8192,24]{0,1:T(8,128)S(1)}, f32[8192,24]{0,1:T(8,128)}, u32[]{:S(2)}, u32[]{:S(2)}) collective-permute-start(f32[8192,24]{0,1:T(8,128)S(1)} %fusion), channel_id=1, source_target_pairs={{0,1},{1,2},{2,3},{3,4},{4,5},{5,6},{6,7},{7,8},{8,9},{9,10},{10,1... | collective-permute-start | bytes 2359304
  2131.9 203.4 %copy-start.1 = (bf16[1,1024,1152]{2,1,0:T(8,128)(2,1)S(1)}, bf16[1,1024,1152]{2,1,0:T(8,128)(2,1)}, u32[]{:S(2)}) copy-start(bf16[1,1024,1152]{2,1,0:T(8,128)(2,1)} %param.10) | copy-start | bytes 7077892
Sparse Core Ops, SparseCore 0:
  11.3 744.1 all-gather.2
  932.9 21.9 all-reduce.9
  1063.0 38.8 all-reduce.11
where the time goes:
time: 2360 us; the launch traced here: 2340 us
  blocking collectives  1580 us (67%)
  starting transfers between devices  278 us (12%)
  local copies, waits for them, and re-layouts  244 us (10%)
  matrix products  116 us (5%)
  waiting for transfers between devices  61.2 us (3%)
  other arithmetic  41.7 us (2%)
    unnamed x3, blocking collectives  1390 us
    unnamed x32, starting transfers between devices  278 us
    unnamed x46, local copies, waits for them, and re-layouts  229 us
    psum x1, blocking collectives, device_step(): loss_val = lax.psum(jnp.sum(log_norm - tok_stats[1]), 'fsdp') / total_tokens  190 us
    unnamed x35, waiting for transfers between devices  61.2 us
  transfers between devices with their start and end apart: 35, of which 3 were waited for; matrix products, arithmetic and copies ran while one was open for 66% of the time, Pallas kernels for 0%

commit v1 on v0

v1 whole, which is shorter than its diff:
```python
import math
import jax
import jax.numpy as jnp
from jax import lax
from jax.sharding import PartitionSpec as P

SOFT_CAP = 30.0
NORM_EPS = 1e-6
XN = 4


def solution(mesh):
    fsdp_size = mesh.shape["fsdp"]
    groups = fsdp_size // XN
    x_groups = [[i * XN + j for j in range(XN)] for i in range(groups)]

    def device_step(emb_shard, tok_ids, lab_ids, h_last, g_embed, norm_w):
        vocab_rows, cols = emb_shard.shape
        batch_loc, seq_len, width = h_last.shape
        tok_count = batch_loc * seq_len
        total_tokens = tok_count * fsdp_size
        quarter = vocab_rows // XN
        row_start = lax.axis_index("tp") * vocab_rows
        me = lax.axis_index("fsdp")
        vocab_iota = jnp.arange(vocab_rows, dtype=jnp.int32)
        emb_scale = jnp.asarray(math.sqrt(width), jnp.bfloat16).astype(jnp.float32)

        piece = emb_shard.T.astype(jnp.bfloat16).reshape(cols, XN, quarter).transpose(1, 0, 2)
        piece = lax.all_to_all(piece, "fsdp", split_axis=0, concat_axis=0, axis_index_groups=x_groups)
        piece = piece.reshape(XN * cols, quarter)
        table = lax.all_gather(piece, "fsdp", axis=0)
        table = table.reshape(groups, XN, XN * cols, quarter).transpose(0, 2, 1, 3).reshape(width, vocab_rows)

        tok_local = tok_ids.reshape(tok_count) - row_start
        tok_hit = (tok_local[:, None] == vocab_iota[None, :]).astype(jnp.bfloat16)
        row_vals = jnp.einsum("tv,dv->td", tok_hit, table, preferred_element_type=jnp.float32).astype(jnp.bfloat16)
        row_vals = lax.psum(row_vals, "tp")
        x_emb = (row_vals.astype(jnp.float32) * emb_scale).astype(jnp.bfloat16)

        mine = jnp.where(lax.axis_index("tp") == 0, norm_w, 0.0)
        norm_full = lax.dynamic_update_slice(jnp.zeros((width,), jnp.float32), mine, (me * cols,))
        norm_gain = 1.0 + lax.psum(norm_full, ("tp", "fsdp"))
        h_wide = h_last.reshape(tok_count, width).astype(jnp.float32)
        inv_rms = lax.rsqrt(jnp.mean(h_wide * h_wide, axis=1, keepdims=True) + NORM_EPS)
        h_norm = h_wide * inv_rms
        x_norm = (h_norm * norm_gain).astype(jnp.bfloat16)

        logits = jnp.einsum("td,dv->tv", x_norm, table, preferred_element_type=jnp.float32)
        tanh_z = jnp.tanh(logits / SOFT_CAP)
        capped = SOFT_CAP * tanh_z
        exp_shift = jnp.exp(capped - SOFT_CAP)
        lab_hit = (lab_ids.reshape(tok_count) - row_start)[:, None] == vocab_iota[None, :]
        tok_stats = jnp.stack([jnp.sum(exp_shift, axis=1), jnp.sum(jnp.where(lab_hit, capped, 0.0), axis=1)])
        tok_stats = lax.psum(tok_stats, "tp")
        sum_exp = tok_stats[0]
        log_norm = jnp.log(sum_exp) + SOFT_CAP
        loss_part = 0.5 * jnp.sum(log_norm - tok_stats[1])

        soft_prob = exp_shift / sum_exp[:, None]
        d_logits = ((soft_prob - lab_hit.astype(jnp.float32)) * (1.0 - tanh_z * tanh_z) / total_tokens).astype(jnp.bfloat16)
        d_part = jnp.einsum("tv,dv->td", d_logits, table, preferred_element_type=jnp.float32)
        d_xnorm = lax.psum(d_part, "tp")
        g_dir = d_xnorm * norm_gain
        d_hidden = (inv_rms * (g_dir - h_norm * jnp.mean(g_dir * h_norm, axis=1, keepdims=True))).astype(jnp.bfloat16)
        small = jnp.concatenate([jnp.sum(d_part * h_norm, axis=0), loss_part[None]])
        small = lax.psum(small, ("tp", "fsdp"))
        loss_val = small[width] / total_tokens
        d_norm_w = lax.dynamic_slice(small, (me * cols,), (cols,))

        both_l = jnp.concatenate([d_logits, (tok_hit * emb_scale.astype(jnp.bfloat16))], axis=0)
        both_x = jnp.concatenate([x_norm, g_embed.reshape(tok_count, width)], axis=0)
        grad = jnp.einsum("tv,td->dv", both_l, both_x, preferred_element_type=jnp.float32)
        grad = grad.reshape(groups, XN * cols, XN, quarter).transpose(0, 2, 1, 3).reshape(fsdp_size, XN * cols, quarter)
        grad = lax.psum_scatter(grad, "fsdp", scatter_dimension=0)
        grad = lax.all_to_all(grad.reshape(XN, cols, quarter), "fsdp", split_axis=0, concat_axis=0, axis_index_groups=x_groups)
        d_table = grad.transpose(1, 0, 2).reshape(cols, vocab_rows).T
        return (x_emb.reshape(batch_loc, seq_len, width), loss_val, d_hidden.reshape(batch_loc, seq_len, width), d_norm_w, d_table)

    spec_tok = P("fsdp", None)
    spec_act = P("fsdp", None, None)
    return jax.shard_map(device_step, mesh=mesh, in_specs=(P("tp", "fsdp"), spec_tok, spec_tok, spec_act, spec_act, P("fsdp")), out_specs=(spec_act, P(), spec_act, P("fsdp"), P("tp", "fsdp")), check_vma=False)
```

time: 2360 us -> 825 us (0.35)
  blocking collectives: 1580 us -> 149 us
  starting transfers between devices: 278 us -> 3.66 us
  waiting for transfers between devices: 61.2 us -> 327 us
  local copies, waits for them, and re-layouts: 244 us -> 129 us
  matrix products: 116 us -> 142 us
    unnamed x3 -> x0, blocking collectives: 1390 us -> none
    unnamed x32 -> x0, starting transfers between devices: 278 us -> none
    reduce_scatter x0 -> x1, waiting for transfers between devices: none -> 238 us  [device_step(): grad = lax.psum_scatter(grad, 'fsdp', scatter_dimension=0)]
    unnamed x46 -> x17, local copies, waits for them, and re-layouts: 229 us -> 17.5 us
    reshape x0 -> x5, local copies, waits for them, and re-layouts: none -> 107 us  [the longest x2 85 us: device_step(): grad.reshape(groups, XN * cols, XN, quarter).transpose(0, 2, 1, 3)]
    unnamed x35 -> x4, waiting for transfers between devices: 61.2 us -> 0.07 us
    psum x1 -> x2, blocking collectives: 190 us -> 134 us  [the longest x1 67.2 us: device_step(): small = lax.psum(small, ('tp', 'fsdp'))]
    psum x2, waiting for transfers between devices: 0.01 us -> 47.7 us  [the longest x1 26.4 us: device_step(): d_xnorm = lax.psum(d_part, 'tp')]
  transfers between devices with their start and end apart: 35 -> 5, of which waited for: 3 -> 4; matrix products, arithmetic and copies ran while one was open for 66% -> 6% of each run, Pallas kernels for 0% -> 0%
where the time goes in v1:
time: 825 us; the launch traced here: 819 us
  waiting for transfers between devices  327 us (40%)
  blocking collectives  149 us (18%)
  matrix products  142 us (17%)
  local copies, waits for them, and re-layouts  129 us (16%)
  other arithmetic  51.4 us (6%)
  between operations  16.5 us (2%)
    reduce_scatter x1, waiting for transfers between devices, device_step(): grad = lax.psum_scatter(grad, 'fsdp', scatter_dimension=0)  238 us
    reshape x2, local copies, waits for them, and re-layouts, device_step(): grad.reshape(groups, XN * cols, XN, quarter).transpose(0, 2, 1, 3)  85 us
    psum x1, blocking collectives, device_step(): small = lax.psum(small, ('tp', 'fsdp'))  67.2 us
    psum x1, blocking collectives, device_step(): norm_gain = 1.0 + lax.psum(norm_full, ('tp', 'fsdp'))  67 us
    dot_general x1, matrix products, device_step(): jnp.einsum('tv,td->dv', both_l, both_x, preferred_element_type=jnp.float32)  46.3 us
    all_gather x1, waiting for transfers between devices, device_step(): table = lax.all_gather(piece, 'fsdp', axis=0)  40.5 us
    dot_general x1, matrix products, device_step(): jnp.einsum('td,dv->tv', x_norm, table, preferred_element_type=jnp.float32)  37.1 us
    dot_general x1, matrix products, device_step(): jnp.einsum('tv,dv->td', tok_hit, table, preferred_element_type=jnp.float32)  31.5 us
  transfers between devices with their start and end apart: 5, of which 4 were waited for; matrix products, arithmetic and copies ran while one was open for 6% of the time, Pallas kernels for 0%

profile of v1, /device:TPU:0, one launch (start us, length us, event | category | flops | bytes accessed | tf_op | source)
XLA Modules:
  0.0 818.6 jit_solution(6990943434550390807)
XLA Ops:
  7.2 0.0 all-gather.2.cloned.1.call-start
  7.2 1.2 convert_bitcast_fusion.1
  8.4 0.2 reshape.86
  8.6 0.2 copy.25
  8.7 12.3 %all_to_all.10 = bf16[4,18,2048]{2,1,0:T(8,128)(2,1)S(1)} all-to-all(bf16[4,18,2048]{2,1,0:T(8,128)(2,1)S(1)} %bitcast.79), channel_id=1, replica_groups={{0,1,2,3},{4,5,6,7},{8,9,10,11},{12,13,14,15},{16,17,18,19},{20,21,22,2..., dimensions={0} | all-to-all | bytes 589824 | tf_op jit(solution)/shard_map/all_to_all | solution.py:29
  21.1 0.8 all_gather_reshape.3
  21.9 0.0 all-gather.2.cloned.1.call-update
  21.9 0.0 all-reduce.5.cloned.1.call-start
  22.0 0.8 fusion.34
  22.8 67.0 %psum.36 = f32[1152]{0:T(1024)S(1)} all-reduce(f32[1152]{0:T(1024)S(1)} %fusion.34), channel_id=1, replica_groups=mesh['tp'=2,'fsdp'=64] {'tp','fsdp'}, use_global_device_ids=true, to_apply=%region_2.3 | all-reduce | flops 1152 | bytes 9216 | tf_op jit(solution)/shard_map/psum | solution.py:42
  89.8 2.2 fusion.20
  92.0 0.7 broadcast_subtract_fusion
  92.7 40.5 %all-gather.2.cloned.1.call-done = bf16[64,72,2048]{2,1,0:T(8,128)(2,1)} async-done(((bf16[1,72,2048]{2,1,0:T(8,128)(2,1)}), bf16[64,72,2048]{2,1,0:T(8,128)(2,1)}) %all-gather.2.cloned.1.call-update) | async-done | bytes 18874384 | tf_op jit(solution)/shard_map/all_gather | solution.py:31
  133.2 21.3 %copy.19 = bf16[16,4,72,2048]{3,1,2,0:T(4,128)(2,1)S(1)} copy(bf16[16,4,72,2048]{3,2,1,0:T(8,128)(2,1)} %bitcast.76) | data formatting | bytes 37748736 | tf_op jit(solution)/shard_map/reshape | solution.py:32
  154.5 15.9 %copy.22 = bf16[144,8,4,2048]{3,1,2,0:T(8,128)(2,1)} copy(bf16[144,8,4,2048]{3,2,1,0:T(4,128)(2,1)S(1)} %bitcast.72) | data formatting | bytes 37748736
  170.4 37.1 %fusion.6 = (f32[1024]{0:T(1024)S(1)}, f32[1024]{0:T(1024)S(1)}, f32[1024,8192]{1,0:T(8,128)}) fusion(s32[1024]{0:T(1024)S(1)} %bitcast.86, bf16[1152,8192]{1,0:T(8,128)(2,1)} %bitcast.73, bf16[1,1024,1152]{2,1,0:T(8,128)(2,1)} %param.9, f32[1152]{0:T(1024)S(1)} %broadcast_add_fusion, f32[1024]{0:T(1024)S(1)} %add_rsqrt_fusion), kind=kOutput, calls=%fused_computation.12 | convolution fusion | flops 19390791680 | bytes 54809088 | tf_op jit(solution)/shard_map/td,dv->tv/dot_general | solution.py:48
  207.5 2.9 psum.37
  210.4 0.6 fusion.36
  211.0 0.0 copy-start.2
  211.0 0.0 copy-start.1
  211.0 26.2 %multiply_convert_fusion = bf16[1024,8192]{1,0:T(8,128)(2,1)} fusion(f32[1024,8192]{1,0:T(8,128)} %get-tuple-element.13, f32[1024]{0:T(1024)S(1)} %bitcast.81, s32[1024]{0:T(1024)S(1)} %bitcast.87), kind=kLoop, calls=%fused_computation.4 | loop fusion | flops 100663296 | bytes 50339840 | tf_op jit(solution)/shard_map/convert_element_type | solution.py:60
  237.2 0.0 copy-done.2
  237.2 0.0 copy-done.1
  237.2 27.0 %fusion.37 = f32[1024,1152]{1,0:T(8,128)} fusion(bf16[1024,8192]{1,0:T(8,128)(2,1)} %multiply_convert_fusion, bf16[1152,8192]{1,0:T(8,128)(2,1)S(1)} %bitcast.75), kind=kOutput, calls=%fused_computation.56 | convolution fusion | flops 19327352832 | bytes 40370176 | tf_op jit(solution)/shard_map/tv,dv->td/dot_general | solution.py:61
  264.2 0.0 copy-start
  264.2 0.0 all-reduce.5.cloned.1.call-update
  264.2 0.0 reduce-scatter.2.cloned.1.call-start
  264.3 6.4 fusion.4
  270.6 26.4 %all-reduce.5.cloned.1.call-done = f32[1024,1152]{1,0:T(8,128)} async-done(((f32[1024,1152]{1,0:T(8,128)}), f32[1024,1152]{1,0:T(8,128)}) %all-reduce.5.cloned.1.call-update) | async-done | bytes 4718608 | tf_op jit(solution)/shard_map/psum | solution.py:62
  297.1 0.0 copy-done
  297.1 0.0 copy-start.6
  297.1 5.7 fusion.15
  302.8 4.2 fusion.19
  307.0 0.0 copy-done.6
  307.0 46.3 %fusion = f32[1152,8192]{1,0:T(8,128)} fusion(bf16[1024,8192]{1,0:T(8,128)(2,1)} %fusion.4, bf16[1024,8192]{1,0:T(8,128)(2,1)} %multiply_convert_fusion, bf16[1024,1152]{1,0:T(8,128)(2,1)S(1)} %bitcast.90, bf16[1024,1152]{1,0:T(8,128)(2,1)S(1)} %get-tuple-element.9), kind=kOutput, calls=%fused_computation | convolution fusion | flops 38731251712 | bytes 76021760 | tf_op jit(solution)/shard_map/tv,td->dv/dot_general | solution.py:72
  353.3 44.4 %reshape.92 = f32[16,72,4,2048]{3,2,1,0:T(4,128)} reshape(f32[1152,8192]{1,0:T(8,128)} %fusion) | data formatting | bytes 75497472 | tf_op jit(solution)/shard_map/reshape | solution.py:73
  397.7 40.6 %copy.20 = f32[16,72,4,2048]{3,1,2,0:T(8,128)} copy(f32[16,72,4,2048]{3,2,1,0:T(4,128)} %reshape.92) | data formatting | bytes 75497472 | tf_op jit(solution)/shard_map/reshape | solution.py:73
  438.3 0.0 reduce-scatter.2.cloned.1.call-update
  438.3 0.0 copy-start.3
  438.3 0.0 copy-start.5
  438.3 0.0 copy-start.4
  438.3 0.0 all-reduce.3.cloned.1.call-start
  438.4 31.5 %fusion.26 = bf16[1024,1152]{1,0:T(8,128)(2,1)} fusion(bf16[1152,8192]{1,0:T(8,128)(2,1)} %bitcast.74, s32[1024]{0:T(1024)S(1)} %bitcast.84), kind=kOutput, calls=%fused_computation.35 | convolution fusion | flops 19336921088 | bytes 21237760 | tf_op jit(solution)/shard_map/tv,dv->td/dot_general | solution.py:36
  469.8 0.0 all-reduce.3.cloned.1.call-update
  469.9 0.0 copy-done.3
  469.9 0.0 copy-done.5
  469.9 0.6 subtract_reduce_fusion
  471.1 238.4 %reduce-scatter.2.cloned.1.call-done = f32[1,72,2048]{2,1,0:T(8,128)} async-done(((f32[64,72,2048]{2,1,0:T(8,128)}), f32[1,72,2048]{2,1,0:T(8,128)}) %reduce-scatter.2.cloned.1.call-update) | async-done | bytes 589840 | tf_op jit(solution)/shard_map/reduce_scatter | solution.py:74
  709.5 2.0 reshape_reduce_scatter.3
  711.5 3.5 all-to-all-start.1
  715.0 21.3 %all-reduce.3.cloned.1.call-done = bf16[1024,1152]{1,0:T(8,128)(2,1)} async-done(((bf16[1024,1152]{1,0:T(8,128)(2,1)}), bf16[1024,1152]{1,0:T(8,128)(2,1)}) %all-reduce.3.cloned.1.call-update) | async-done | bytes 2359312 | tf_op jit(solution)/shard_map/psum | solution.py:37
  736.3 3.5 fusion.27
  739.8 0.0 copy-done.4
  739.8 67.2 %psum.38 = f32[1153]{0:T(1024)S(1)} all-reduce(f32[1153]{0:T(1024)S(1)} %pad_maximum_fusion.1), channel_id=1, replica_groups=mesh['tp'=2,'fsdp'=64] {'tp','fsdp'}, use_global_device_ids=true, to_apply=%region_8.9 | all-reduce | flops 1153 | bytes 9224 | tf_op jit(solution)/shard_map/psum | solution.py:66
  807.0 0.5 slice.14
  807.6 0.6 dynamic_slice.3
  808.8 0.0 all-to-all-done.1
  808.8 0.4 copy.21
  809.2 0.2 pad.8
  809.4 1.3 copy.23
  (6 shorter events, 0.0 us)
Async XLA Ops:
  7.2 126.0 %all-gather.2.cloned.1.call-start = ((), (), s32[]{:S(2)}) async-start(), calls=%async_computation.3 | async-start | bytes 19169280 | tf_op jit(solution)/shard_map/all_gather | solution.py:31
  21.9 275.2 %all-reduce.5.cloned.1.call-start = ((), (), s32[]{:S(2)}) async-start(), calls=%async_computation.5 | async-start | bytes 9437184 | tf_op jit(solution)/shard_map/psum | solution.py:62
  211.0 26.2 %copy-start.2 = (f32[1,1024]{1,0:T(1,128)}, f32[1,1024]{1,0:T(1,128)S(1)}, u32[]{:S(2)}) copy-start(f32[1,1024]{1,0:T(1,128)S(1)} %get-tuple-element.11) | copy-start | bytes 12292
  211.0 26.2 %copy-start.1 = (bf16[144,8,4,2048]{3,1,2,0:T(8,128)(2,1)S(1)}, bf16[144,8,4,2048]{3,1,2,0:T(8,128)(2,1)}, u32[]{:S(2)}) copy-start(bf16[144,8,4,2048]{3,1,2,0:T(8,128)(2,1)} %copy.22) | copy-start | bytes 56623108
  264.2 32.9 %copy-start = (bf16[1,1024,1152]{2,1,0:T(8,128)(2,1)S(1)}, bf16[1,1024,1152]{2,1,0:T(8,128)(2,1)}, u32[]{:S(2)}) copy-start(bf16[1,1024,1152]{2,1,0:T(8,128)(2,1)} %param.9) | copy-start | bytes 7077892
  264.2 445.3 %reduce-scatter.2.cloned.1.call-start = ((), (), s32[]{:S(2)}) async-start(), calls=%async_computation.6 | async-start | bytes 38338560 | tf_op jit(solution)/shard_map/reduce_scatter | solution.py:74
  297.1 9.9 %copy-start.6 = (bf16[1,1024,1152]{2,1,0:T(8,128)(2,1)S(1)}, bf16[1,1024,1152]{2,1,0:T(8,128)(2,1)}, u32[]{:S(2)}) copy-start(bf16[1,1024,1152]{2,1,0:T(8,128)(2,1)} %param.10) | copy-start | bytes 7077892
  438.3 31.6 %copy-start.3 = (f32[1,1024]{1,0:T(1,128)S(1)}, f32[1,1024]{1,0:T(1,128)}, u32[]{:S(2)}) copy-start(f32[1,1024]{1,0:T(1,128)} %copy-done.2) | copy-start | bytes 12292
  438.3 31.6 %copy-start.5 = (f32[1,1024]{1,0:T(1,128)S(1)}, f32[1,1024]{1,0:T(1,128)}, u32[]{:S(2)}) copy-start(f32[1,1024]{1,0:T(1,128)} %get-tuple-element.12) | copy-start | bytes 12292
  438.3 301.5 %copy-start.4 = (f32[1152]{0:T(1024)S(1)}, f32[1152]{0:T(1024)}, u32[]{:S(2)}) copy-start(f32[1152]{0:T(1024)} %get-tuple-element.8) | copy-start | bytes 13828
  438.3 298.0 %all-reduce.3.cloned.1.call-start = ((), (), s32[]{:S(2)}) async-start(), calls=%async_computation.4 | async-start | bytes 4718592 | tf_op jit(solution)/shard_map/psum | solution.py:37
  711.5 97.3 %all-to-all-start.1 = ((f32[4,18,2048]{2,1,0:T(8,128)}), f32[4,18,2048]{2,1,0:T(8,128)S(1)}, u32[]{:S(2)}, u32[]{:S(2)}) async-start(f32[4,18,2048]{2,1,0:T(8,128)} %reshape_reduce_scatter.3), calls=%async_computation.2 | async-start | bytes 1572864 | tf_op jit(solution)/shard_map/all_to_all | solution.py:75
Sparse Core Ops, SparseCore 0:
  22.0 111.1 all-gather.1
  264.3 32.6 all-reduce.4
  438.4 271.0 reduce-scatter.1
  712.4 23.8 all-reduce.2

commit v2 on v1

v2 whole, which is shorter than its diff:
```python
import functools
import math
import jax
import jax.numpy as jnp
from jax import lax
from jax.experimental import pallas as pl
from jax.experimental.pallas import tpu as pltpu
from jax.sharding import PartitionSpec as P

SOFT_CAP = 30.0
NORM_EPS = 1e-6
MESH = pl.DeviceIdType.MESH
NX = 4
COLORS = 3
SLOTS = 3
CHUNKS = 8
ORDERS = (("x", "y", "z"), ("y", "z", "x"), ("z", "x", "y"))
STEP = {"x": 1, "y": 4, "z": 16}
F32, BF16 = jnp.float32, jnp.bfloat16


def coords(me):
    return {"x": lax.rem(me, 4), "y": lax.rem(lax.div(me, 4), 4), "z": lax.div(me, 16)}


def shifted(me, pos, axis, d):
    there = lax.rem(pos[axis] + d, 4)
    return me + (there - pos[axis]) * STEP[axis]


def remote(src, dst, send, recv, device):
    return pltpu.make_async_remote_copy(src_ref=src, dst_ref=dst, send_sem=send, recv_sem=recv, device_id=device, device_id_type=MESH)


def greet(devices):
    barrier = pltpu.get_barrier_semaphore()
    for n in devices:
        pl.semaphore_signal(barrier, inc=1, device_id=n, device_id_type=MESH)
    pl.semaphore_wait(barrier, len(devices))


def grad_kernel(total_tokens, emb_scale, u_ref, table_ref, xt_ref, ids_ref, stat_ref, h_ref, gain_ref, loss_ref,
                grad_ref, dh_ref, small_ref, own, buf2, buf3, ra0, ra1, ra2, rb, rc, ubuf, tbuf, dz, dxn, dxn_in, sums, sums_in,
                load_sem, ssem, rsem, xsend, xrecv, sum_send, sum_recv, credit):
    me = lax.axis_index("fsdp")
    tp = lax.axis_index("tp")
    pos = coords(me)
    chunks = CHUNKS
    lanes = own.shape[-1]
    rows = own.shape[-2]
    tokens, width = h_ref.shape
    vocab = u_ref.shape[1]
    quarter = vocab // NX
    ra = (ra0, ra1, ra2)
    near = [{"fsdp": shifted(me, pos, a, d)} for a in "xyz" for d in (1, 3)]
    partner = {"tp": 1 - tp}
    greet(near + [{"fsdp": shifted(me, pos, a, 2)} for a in "xyz"] + [partner])

    def loads(i):
        c, q = lax.div(i, NX), lax.rem(i, NX)
        s = lax.rem(i, 2)
        at = pl.ds(pl.multiple_of(q * quarter + c * lanes, 128), lanes)
        return (pltpu.make_async_copy(u_ref.at[:, at], ubuf.at[s], load_sem.at[s, 0]),
                pltpu.make_async_copy(table_ref.at[:, at], tbuf.at[s], load_sem.at[s, 1]))

    def produce(c, slot):
        def one(q, carry):
            i = c * NX + q
            s = lax.rem(i, 2)
            for cp in loads(i):
                cp.wait()

            @pl.when(i + 1 < chunks * NX)
            def _():
                for cp in loads(i + 1):
                    cp.start()

            first_id = q * quarter + c * lanes

            def block(b, carry):
                r = pl.ds(pl.multiple_of(b * 256, 256), 256)
                ids = lax.broadcasted_iota(jnp.int32, (256, lanes), 1) + first_id
                u = ubuf[s, r]
                prob = jnp.exp(SOFT_CAP * u - stat_ref[r, 0:1])
                hit = (ids_ref[r, 1:2] == ids).astype(F32)
                d = ((prob - hit) * (1.0 - u * u) / total_tokens).astype(BF16)
                dz[r] = d
                dz[pl.ds(pl.multiple_of(tokens + b * 256, 256), 256)] = jnp.where(ids_ref[r, 0:1] == ids, emb_scale, 0.0).astype(BF16)
                part = lax.dot_general(d, tbuf[s], (((1,), (1,)), ((), ())), preferred_element_type=F32)
                dxn[r] = dxn[r] + part
                return carry

            lax.fori_loop(0, tokens // 256, block, 0)

            def out(z, carry):
                w = width // 4
                v = jnp.dot(xt_ref[pl.ds(pl.multiple_of(z * w, 32), w), :], dz[...], preferred_element_type=F32)
                own[slot, q, z] = v.reshape(4, COLORS, rows, lanes)
                return carry

            lax.fori_loop(0, 4, out, 0)
            return carry

        lax.fori_loop(0, NX, one, 0)

    def own_at(s, k, a1, half):
        o = ORDERS[k]
        sel = {o[0]: a1, o[1]: pl.ds(2 * half, 2), o[2]: slice(None)}
        return own.at[s, sel["x"], sel["z"], sel["y"], k]

    def part(phase, k, s, a, half):
        if phase == 0:
            return own_at(s, k, a, half)
        if phase == 1:
            return buf2.at[s, k, a, pl.ds(2 * half, 2)]
        return buf3.at[s, k, a, :, pl.ds(128 * half, 128)]

    def land(phase, k, s, m):
        return ra[k].at[s, m] if phase == 0 else (rb, rc)[phase - 1].at[s, k, m]

    def copies(phase, k, s, step):
        axis = ORDERS[k][phase]
        p = pos[axis]
        right, left, far = lax.rem(p + 1, 4), lax.rem(p + 3, 4), lax.rem(p + 2, 4)
        to_r, to_l = {"fsdp": shifted(me, pos, axis, 1)}, {"fsdp": shifted(me, pos, axis, 3)}
        if step == 0:
            table = ((0, part(phase, k, s, far, 0), to_r), (1, part(phase, k, s, far, 1), to_l),
                     (2, part(phase, k, s, right, 1), to_r), (3, part(phase, k, s, left, 0), to_l))
        else:
            table = ((4, land(phase, k, s, 0), to_r), (5, land(phase, k, s, 1), to_l))
        return [(m, remote(src, land(phase, k, s, m), ssem.at[phase, s, k, m], rsem.at[phase, s, k, m], dev)) for m, src, dev in table]

    def first(phase, s):
        for k in range(COLORS):
            for _, cp in copies(phase, k, s, 0):
                cp.start()

    def second(phase, s):
        for k in range(COLORS):
            axis = ORDERS[k][phase]
            p = pos[axis]
            right, left = lax.rem(p + 1, 4), lax.rem(p + 3, 4)
            one = copies(phase, k, s, 0)
            for m, a in ((0, right), (1, left)):
                one[m][1].wait_recv()
                dst = land(phase, k, s, m)
                dst[...] = dst[...] + part(phase, k, s, a, m)[...]
            for _, cp in copies(phase, k, s, 1):
                cp.start()

    def last(phase, s, store):
        for k in range(COLORS):
            p = pos[ORDERS[k][phase]]
            one, two = copies(phase, k, s, 0), copies(phase, k, s, 1)
            for m, cp in one[2:] + two:
                cp.wait_recv()
            for half, (m, n) in enumerate(((4, 3), (5, 2))):
                store(k, half, part(phase, k, s, p, half)[...] + land(phase, k, s, m)[...] + land(phase, k, s, n)[...])
            for m, cp in one + two:
                cp.wait_send()

    def store1(s):
        def put(k, half, v):
            if k == 2:
                for i in range(2):
                    buf2[s, k, 2 * half + i] = v[i]
            else:
                for i in range(2):
                    buf2[s, k, 2 * half + i] = v[:, i]
        return put

    def store2(s):
        def put(k, half, v):
            buf3[s, k, pl.ds(2 * half, 2)] = v
        return put

    def store3(c):
        def put(k, half, v):
            grad_ref[k, :, pl.ds(pl.multiple_of(c * lanes + 128 * half, 128), 128)] = v
        return put

    half_rows = tokens // 2
    mine = pl.ds(pl.multiple_of(tp * half_rows, half_rows), half_rows)
    other = pl.ds(pl.multiple_of((1 - tp) * half_rows, half_rows), half_rows)

    def swap_dxn():
        return remote(dxn.at[other], dxn_in, xsend.at[0], xrecv.at[0], partner)

    def swap_dh():
        return remote(dh_ref.at[mine], dh_ref.at[mine], xsend.at[1], xrecv.at[1], partner)

    def finish_hidden():
        swap_dxn().wait()
        sums[...] = jnp.zeros_like(sums)
        gain = gain_ref[...]

        def block(b, acc):
            lo = pl.ds(pl.multiple_of(b * 128, 128), 128)
            r = pl.ds(pl.multiple_of(tp * half_rows + b * 128, 128), 128)
            inv = stat_ref[r, 1:2]
            hn = h_ref[r].astype(F32) * inv
            dx = dxn[r] + dxn_in[lo]
            g_dir = dx * gain
            mean = jnp.mean(g_dir * hn, axis=1, keepdims=True)
            dh_ref[r] = (inv * (g_dir - hn * mean)).astype(BF16)
            return acc + jnp.sum(dx * hn, axis=0, keepdims=True)

        dg = lax.fori_loop(0, half_rows // 128, block, jnp.zeros((1, width), F32))
        n = width // 128
        for i in range(n):
            sums[pl.ds(i, 1), :] = dg[:, 128 * i:128 * i + 128]
        sums[pl.ds(n, 1), :] = loss_ref[...]
        swap_dh().start()

    def sum_copies(phase):
        if phase == 3:
            peers = [partner]
        else:
            peers = [{"fsdp": shifted(me, pos, "xyz"[phase], d)} for d in (1, 2, 3)]
        return [remote(sums, sums_in.at[phase, j], sum_send.at[phase, j], sum_recv.at[phase, j], n) for j, n in enumerate(peers)]

    def sum_start(phase):
        for cp in sum_copies(phase):
            cp.start()

    def sum_end(phase):
        cps = sum_copies(phase)
        for cp in cps:
            cp.wait()
        if phase == 3:
            small_ref[...] = sums[...] + sums_in[3, 0]
        else:
            sums[...] = sums[...] + sums_in[phase, 0] + sums_in[phase, 1] + sums_in[phase, 2]

    dxn[...] = jnp.zeros_like(dxn)
    for cp in loads(0):
        cp.start()
    ticks = chunks + 6

    def tick(t, carry):
        @pl.when(t < chunks)
        def _():
            produce(t, lax.rem(t, SLOTS))

        @pl.when(t >= 1)
        def _():
            for i in range(6):
                pl.semaphore_wait(credit.at[i], 1)

        def stage(delay, run):
            c = t - delay
            @pl.when(jnp.logical_and(c >= 0, c < chunks))
            def _():
                run(c, lax.rem(c, SLOTS))

        def s2(c, s):
            last(0, s, store1(s))
            first(1, s)

        def s4(c, s):
            last(1, s, store2(s))
            first(2, s)

        stage(0, lambda c, s: first(0, s))
        @pl.when(t == chunks - 1)
        def _():
            swap_dxn().start()
        stage(6, lambda c, s: last(2, s, store3(c)))
        stage(5, lambda c, s: second(2, s))
        stage(4, s4)
        stage(3, lambda c, s: second(1, s))
        stage(2, s2)
        stage(1, lambda c, s: second(0, s))

        @pl.when(t == chunks)
        def _():
            finish_hidden()
        @pl.when(t == chunks + 1)
        def _():
            sum_start(0)
            swap_dh().wait()
        for phase in range(3):
            @pl.when(t == chunks + 2 + phase)
            def _():
                sum_end(phase)
                sum_start(phase + 1)
        @pl.when(t == chunks + 5)
        def _():
            sum_end(3)

        @pl.when(t < ticks - 1)
        def _():
            for i, n in enumerate(near):
                pl.semaphore_signal(credit.at[i], inc=1, device_id=n, device_id_type=MESH)
        return carry

    lax.fori_loop(0, ticks, tick, 0)


def gradients(total_tokens, emb_scale, u, table, xt, ids, stat, h, gain, loss):
    tokens, vocab = u.shape
    width = h.shape[1]
    quarter = vocab // NX
    lanes = quarter // CHUNKS
    rows = width // 48
    vm = pl.BlockSpec(memory_space=pltpu.VMEM)
    hbm = pl.BlockSpec(memory_space=pl.ANY)
    dma = pltpu.SemaphoreType.DMA
    return pl.pallas_call(
        functools.partial(grad_kernel, total_tokens, emb_scale),
        out_shape=[jax.ShapeDtypeStruct((COLORS, rows, quarter), F32), jax.ShapeDtypeStruct((tokens, width), BF16), jax.ShapeDtypeStruct((16, 128), F32)],
        in_specs=[hbm, hbm] + [vm] * 6,
        out_specs=[vm, vm, vm],
        scratch_shapes=[
            pltpu.VMEM((SLOTS, 4, 4, 4, COLORS, rows, lanes), F32),
            pltpu.VMEM((SLOTS, COLORS, 4, 4, rows, lanes), F32),
            pltpu.VMEM((SLOTS, COLORS, 4, rows, lanes), F32),
            pltpu.VMEM((SLOTS, 6, 4, 2, rows, lanes), F32),
            pltpu.VMEM((SLOTS, 6, 4, 2, rows, lanes), F32),
            pltpu.VMEM((SLOTS, 6, 2, 4, rows, lanes), F32),
            pltpu.VMEM((SLOTS, COLORS, 6, 2, rows, lanes), F32),
            pltpu.VMEM((SLOTS, COLORS, 6, rows, 128), F32),
            pltpu.VMEM((2, tokens, lanes), F32),
            pltpu.VMEM((2, width, lanes), BF16),
            pltpu.VMEM((2 * tokens, lanes), BF16),
            pltpu.VMEM((tokens, width), F32),
            pltpu.VMEM((tokens // 2, width), F32),
            pltpu.VMEM((16, 128), F32),
            pltpu.VMEM((4, 3, 16, 128), F32),
            dma((2, 2)),
            dma((3, SLOTS, COLORS, 6)),
            dma((3, SLOTS, COLORS, 6)),
            dma((2,)),
            dma((2,)),
            dma((4, 3)),
            dma((4, 3)),
            pltpu.SemaphoreType.REGULAR((6,)),
        ],
        compiler_params=pltpu.CompilerParams(collective_id=2, has_side_effects=True, vmem_limit_bytes=63 * 2**20),
    )(u, table, xt, ids, stat, h, gain, loss)


def math_scale(width):
    import numpy as np
    return float(np.asarray(math.sqrt(width), BF16).astype(np.float32))


def solution(mesh):
    fsdp_size = mesh.shape["fsdp"]
    groups = fsdp_size // NX
    x_groups = [[i * NX + j for j in range(NX)] for i in range(groups)]

    def device_step(emb_shard, tok_ids, lab_ids, h_last, g_embed, norm_w):
        vocab_rows, cols = emb_shard.shape
        batch_loc, seq_len, width = h_last.shape
        tok_count = batch_loc * seq_len
        total_tokens = tok_count * fsdp_size
        quarter = vocab_rows // NX
        row_start = lax.axis_index("tp") * vocab_rows
        me = lax.axis_index("fsdp")
        vocab_iota = jnp.arange(vocab_rows, dtype=jnp.int32)
        emb_scale = jnp.asarray(math.sqrt(width), jnp.bfloat16).astype(jnp.float32)

        piece = emb_shard.T.astype(jnp.bfloat16).reshape(cols, NX, quarter).transpose(1, 0, 2)
        piece = lax.all_to_all(piece, "fsdp", split_axis=0, concat_axis=0, axis_index_groups=x_groups)
        piece = piece.reshape(NX * cols, quarter)
        table = lax.all_gather(piece, "fsdp", axis=0)
        table = table.reshape(groups, NX, NX * cols, quarter).transpose(0, 2, 1, 3).reshape(width, vocab_rows)

        tok_local = tok_ids.reshape(tok_count) - row_start
        tok_hit = (tok_local[:, None] == vocab_iota[None, :]).astype(jnp.bfloat16)
        row_vals = jnp.einsum("tv,dv->td", tok_hit, table, preferred_element_type=jnp.float32).astype(jnp.bfloat16)
        row_vals = lax.psum(row_vals, "tp")
        x_emb = (row_vals.astype(jnp.float32) * emb_scale).astype(jnp.bfloat16)

        mine = jnp.where(lax.axis_index("tp") == 0, norm_w, 0.0)
        norm_full = lax.dynamic_update_slice(jnp.zeros((width,), jnp.float32), mine, (me * cols,))
        norm_gain = 1.0 + lax.psum(norm_full, ("tp", "fsdp"))
        h_wide = h_last.reshape(tok_count, width).astype(jnp.float32)
        inv_rms = lax.rsqrt(jnp.mean(h_wide * h_wide, axis=1, keepdims=True) + NORM_EPS)
        h_norm = h_wide * inv_rms
        x_norm = (h_norm * norm_gain).astype(jnp.bfloat16)

        logits = jnp.einsum("td,dv->tv", x_norm, table, preferred_element_type=jnp.float32)
        tanh_z = jnp.tanh(logits / SOFT_CAP)
        capped = SOFT_CAP * tanh_z
        exp_shift = jnp.exp(capped - SOFT_CAP)
        lab_hit = (lab_ids.reshape(tok_count) - row_start)[:, None] == vocab_iota[None, :]
        tok_stats = jnp.stack([jnp.sum(exp_shift, axis=1), jnp.sum(jnp.where(lab_hit, capped, 0.0), axis=1)])
        tok_stats = lax.psum(tok_stats, "tp")
        sum_exp = tok_stats[0]
        log_norm = jnp.log(sum_exp) + SOFT_CAP
        loss_part = 0.5 * jnp.sum(log_norm - tok_stats[1])

        xt = jnp.concatenate([x_norm.T, g_embed.reshape(tok_count, width).T], axis=1)
        ids = jnp.stack([tok_local, lab_ids.reshape(tok_count) - row_start], axis=1)
        stat = jnp.concatenate([log_norm[:, None], inv_rms], axis=1)
        grad, d_hidden, small = gradients(total_tokens, math_scale(width), tanh_z, table, xt, ids, stat, h_last.reshape(tok_count, width), norm_gain[None, :], jnp.full((1, 128), loss_part))
        loss_val = small[width // 128, 0] / total_tokens
        d_norm_w = lax.dynamic_slice(small.reshape(-1), (me * cols,), (cols,))
        grad = lax.all_to_all(grad.reshape(NX, cols, quarter), "fsdp", split_axis=0, concat_axis=0, axis_index_groups=x_groups)
        d_table = grad.transpose(1, 0, 2).reshape(cols, vocab_rows).T
        return (x_emb.reshape(batch_loc, seq_len, width), loss_val, d_hidden.reshape(batch_loc, seq_len, width), d_norm_w, d_table)

    spec_tok = P("fsdp", None)
    spec_act = P("fsdp", None, None)
    return jax.shard_map(device_step, mesh=mesh, in_specs=(P("tp", "fsdp"), spec_tok, spec_tok, spec_act, spec_act, P("fsdp")), out_specs=(spec_act, P(), spec_act, P("fsdp"), P("tp", "fsdp")), check_vma=False)
```

time: 825 us -> 459 us (0.56)
  waiting for transfers between devices: 327 us -> 39.3 us
  Pallas kernels: 0 us -> 182 us
  matrix products: 142 us -> 68.1 us
  local copies, waits for them, and re-layouts: 129 us -> 56.1 us
  blocking collectives: 149 us -> 82.1 us
  other arithmetic: 51.4 us -> 9.93 us
    reduce_scatter x1 -> x0, waiting for transfers between devices: 238 us -> none  [device_step(): grad = lax.psum_scatter(grad, 'fsdp', scatter_dimension=0)]
    pallas_call x0 -> x1, Pallas kernels: none -> 182 us  [gradients(): pl.pallas_call(functools.partial(grad_kernel, total_tokens, emb_scale), o...]
    reshape x5 -> x3, local copies, waits for them, and re-layouts: 107 us -> 2.36 us  [the longest x1 2.02 us: device_step(): grad.reshape(NX, cols, quarter)]
    dot_general x2 -> x0, matrix products: 73.3 us -> none  [the longest x1 46.3 us: device_step(): jnp.einsum('tv,td->dv', both_l, both_x, preferred_element_type=jnp.float32)]
    psum x1 -> x0, blocking collectives: 67.2 us -> none  [device_step(): small = lax.psum(small, ('tp', 'fsdp'))]
    convert_element_type x3 -> x1, other arithmetic: 31.5 us -> 1.32 us  [device_step(): emb_shard.T.astype(jnp.bfloat16).reshape(cols, NX, quarter)]
    psum x1 -> x0, waiting for transfers between devices: 26.4 us -> none  [device_step(): d_xnorm = lax.psum(d_part, 'tp')]
    transpose x0 -> x1, local copies, waits for them, and re-layouts: none -> 21.3 us  [device_step(): table.reshape(groups, NX, NX * cols, quarter).transpose(0, 2, 1, 3)]
  transfers between devices with their start and end apart: 5 -> 3, of which waited for: 4 -> 2; matrix products, arithmetic and copies ran while one was open for 6% -> 13% of each run, Pallas kernels for 0% -> 40%
where the time goes in v2:
time: 459 us; the launch traced here: 458 us
  Pallas kernels  182 us (40%)
  blocking collectives  82.1 us (18%)
  matrix products  68.1 us (15%)
  local copies, waits for them, and re-layouts  56.1 us (12%)
  waiting for transfers between devices  39.3 us (9%)
  between operations  16.6 us (4%)
  other arithmetic  9.93 us (2%)
    pallas_call x1, Pallas kernels, gradients(): pl.pallas_call(functools.partial(grad_kernel, total_tokens, emb_scale), o...  182 us
    psum x1, blocking collectives, device_step(): norm_gain = 1.0 + lax.psum(norm_full, ('tp', 'fsdp'))  67 us
    dot_general x1, matrix products, device_step(): jnp.einsum('td,dv->tv', x_norm, table, preferred_element_type=jnp.float32)  36.5 us
    dot_general x1, matrix products, device_step(): jnp.einsum('tv,dv->td', tok_hit, table, preferred_element_type=jnp.float32)  31.6 us
    all_gather x1, waiting for transfers between devices, device_step(): table = lax.all_gather(piece, 'fsdp', axis=0)  31.4 us
    transpose x1, local copies, waits for them, and re-layouts, device_step(): table.reshape(groups, NX, NX * cols, quarter).transpose(0, 2, 1, 3)  21.3 us
    unnamed x16, local copies, waits for them, and re-layouts  18.8 us
    all_to_all x1, blocking collectives, device_step(): lax.all_to_all(piece, 'fsdp', split_axis=0, concat_axis=0, axis_index_gro...  12.3 us
  transfers between devices with their start and end apart: 3, of which 2 were waited for; matrix products, arithmetic and copies ran while one was open for 13% of the time, Pallas kernels for 40%

profile of v2, /device:TPU:0, one launch (start us, length us, event | category | flops | bytes accessed | tf_op | source)
XLA Modules:
  0.0 458.1 jit_solution(9200688330291391154)
XLA Ops:
  7.2 0.0 copy-start
  7.2 0.0 all-gather.2.cloned.1.call-start
  7.2 1.3 convert_bitcast_fusion
  8.6 0.2 reshape.132
  8.7 0.2 copy.37
  8.9 12.3 %all_to_all.10 = bf16[4,18,2048]{2,1,0:T(8,128)(2,1)S(1)} all-to-all(bf16[4,18,2048]{2,1,0:T(8,128)(2,1)S(1)} %bitcast.56), channel_id=1, replica_groups={{0,1,2,3},{4,5,6,7},{8,9,10,11},{12,13,14,15},{16,17,18,19},{20,21,22,2..., dimensions={0} | all-to-all | bytes 589824 | tf_op jit(solution)/shard_map/all_to_all | solution.py:365
  21.2 0.8 all_gather_reshape.3
  22.0 0.0 all-gather.2.cloned.1.call-update
  22.1 0.0 all-reduce.2.cloned.1.call-start
  22.1 0.8 fusion.14
  22.9 67.0 %psum.22 = f32[1152]{0:T(1024)S(1)} all-reduce(f32[1152]{0:T(1024)S(1)} %fusion.14), channel_id=1, replica_groups=mesh['tp'=2,'fsdp'=64] {'tp','fsdp'}, use_global_device_ids=true, to_apply=%region_2.3 | all-reduce | flops 1152 | bytes 9216 | tf_op jit(solution)/shard_map/psum | solution.py:378
  89.9 0.0 copy-start.3
  89.9 0.6 broadcast_in_dim.27.gain_ref
  90.5 0.0 copy-done
  90.5 0.5 fusion.2
  91.1 0.6 fusion.9
  91.7 0.0 copy-done.3
  91.7 2.5 pad_maximum_fusion
  94.2 0.0 copy-start.4
  94.2 0.0 copy-start.5
  94.2 6.7 %copy.30.xt_ref = bf16[1152,2048]{1,0:T(8,128)(2,1)} copy(bf16[1152,2048]{0,1:T(8,128)(2,1)} %pad_maximum_fusion) | data formatting | bytes 9437184 | tf_op jit(solution)/shard_map/concatenate | solution.py:395
  100.9 0.0 copy-done.4
  100.9 0.0 copy-done.5
  101.0 1.0 copy.31.ids_ref
  102.0 31.4 %all-gather.2.cloned.1.call-done = bf16[64,72,2048]{2,1,0:T(8,128)(2,1)} async-done(((bf16[1,72,2048]{2,1,0:T(8,128)(2,1)}), bf16[64,72,2048]{2,1,0:T(8,128)(2,1)}) %all-gather.2.cloned.1.call-update) | async-done | bytes 18874384 | tf_op jit(solution)/shard_map/all_gather | solution.py:367
  133.4 21.3 %copy.29 = bf16[16,72,4,2048]{3,2,1,0:T(4,128)(2,1)S(1)} copy(bf16[16,72,4,2048]{3,1,2,0:T(8,128)(2,1)} %bitcast.51) | data formatting | bytes 37748736 | tf_op jit(solution)/shard_map/transpose | solution.py:368
  154.7 15.9 %copy.34 = bf16[144,8,4,2048]{3,1,2,0:T(8,128)(2,1)} copy(bf16[144,8,4,2048]{3,2,1,0:T(4,128)(2,1)S(1)} %bitcast.46) | data formatting | bytes 37748736
  170.5 0.0 copy-start.1
  170.5 31.6 %fusion.5 = bf16[1024,1152]{1,0:T(8,128)(2,1)} fusion(bf16[1152,8192]{1,0:T(8,128)(2,1)} %bitcast.47, s32[1024]{0:T(1024)S(1)} %bitcast.62), kind=kOutput, calls=%fused_computation.15 | convolution fusion | flops 19336921088 | bytes 21237760 | tf_op jit(solution)/shard_map/tv,dv->td/dot_general | solution.py:372
  202.1 0.0 all-reduce.2.cloned.1.call-update
  202.2 0.0 copy-done.1
  202.2 36.5 %exponential_reduce_fusion = (f32[1024]{0:T(1024)S(1)}, f32[1024]{0:T(1024)S(1)}, f32[1024,8192]{1,0:T(8,128)}) fusion(s32[1024]{0:T(1024)S(1)} %bitcast.60, bf16[1152,8192]{1,0:T(8,128)(2,1)} %bitcast.48, bf16[1,1024,1152]{2,1,0:T(8,128)(2,1)S(1)} %copy-done.1, f32[1152]{0:T(1024)S(1)} %broadcast_add_fusion, f32[1024]{0:T(1024)S(1)} %add_rsqrt_fusion), kind=kOutput, calls=%fused_computation.2 | convolution fusion | flops 19390791680 | bytes 54809088 | tf_op jit(solution)/shard_map/td,dv->tv/dot_general | solution.py:384
  238.7 2.7 psum.23
  241.4 0.6 fusion.13
  242.0 1.0 copy.32.stat_ref
  243.7 0.5 broadcast_in_dim.28.loss_ref
  244.2 182.2 %shard_map.101 = (f32[3,24,2048]{2,1,0:T(8,128)}, bf16[1024,1152]{1,0:T(8,128)(2,1)}, f32[16,128]{1,0:T(8,128)}) custom-call(f32[1024,8192]{1,0:T(8,128)} %get-tuple-element.15.u_ref, bf16[1152,8192]{1,0:T(8,128)(2,1)} %bitcast.49, bf16[1152,2048]{1,0:T(8,128)(2,1)} %copy.30.xt_ref, s32[1024,2]{1,0:T(8,128)} %copy.31.ids_ref, f32[1024,2]{1,0:T(8,128)} %copy.32.stat_ref, ...), custom_call_target="tpu_custom_call" | custom-call | tf_op jit(solution)/shard_map/pallas_call | solution.py:309
  426.4 2.0 reshape.140
  428.4 3.7 all-to-all-start.1
  432.1 0.0 copy-start.2
  432.1 1.3 slice.11
  433.5 1.3 dynamic_slice.3
  435.4 7.9 %all-to-all-done.1 = f32[4,18,2048]{2,1,0:T(8,128)S(1)} async-done(((f32[4,18,2048]{2,1,0:T(8,128)}), f32[4,18,2048]{2,1,0:T(8,128)S(1)}, u32[]{:S(2)}, u32[]{:S(2)}) %all-to-all-start.1) | async-done | bytes 589856 | tf_op jit(solution)/shard_map/all_to_all | solution.py:401
  443.3 0.4 copy.33
  443.7 0.2 pad.8
  443.8 1.3 copy.35
  445.2 0.0 all-reduce.2.cloned.1.call-done
  445.2 3.5 fusion.6
  448.7 0.0 copy-done.2
  448.7 1.4 copy.41
  (7 shorter events, 0.1 us)
Async XLA Ops:
  7.2 83.4 %copy-start = (bf16[1,1024,1152]{2,1,0:T(8,128)(2,1)S(1)}, bf16[1,1024,1152]{2,1,0:T(8,128)(2,1)}, u32[]{:S(2)}) copy-start(bf16[1,1024,1152]{2,1,0:T(8,128)(2,1)} %param.9) | copy-start | bytes 7077892
  7.2 126.2 %all-gather.2.cloned.1.call-start = ((), (), s32[]{:S(2)}) async-start(), calls=%async_computation.2 | async-start | bytes 19169280 | tf_op jit(solution)/shard_map/all_gather | solution.py:367
  22.1 423.1 %all-reduce.2.cloned.1.call-start = ((), (), s32[]{:S(2)}) async-start(), calls=%async_computation.3 | async-start | bytes 4718592 | tf_op jit(solution)/shard_map/psum | solution.py:373
  89.9 1.8 copy-start.3
  94.2 6.7 %copy-start.4 = (s32[1,1024]{1,0:T(1,128)S(1)}, s32[1,1024]{1,0:T(1,128)}, u32[]{:S(2)}) copy-start(s32[1,1024]{1,0:T(1,128)} %param.8) | copy-start | bytes 12292
  94.2 6.7 %copy-start.5 = (s32[1,1024]{1,0:T(1,128)S(1)}, s32[1,1024]{1,0:T(1,128)}, u32[]{:S(2)}) copy-start(s32[1,1024]{1,0:T(1,128)} %param.7) | copy-start | bytes 12292
  170.5 31.6 %copy-start.1 = (bf16[1,1024,1152]{2,1,0:T(8,128)(2,1)S(1)}, bf16[1,1024,1152]{2,1,0:T(8,128)(2,1)}, u32[]{:S(2)}) copy-start(bf16[1,1024,1152]{2,1,0:T(8,128)(2,1)} %param.9) | copy-start | bytes 7077892
  428.4 14.8 %all-to-all-start.1 = ((f32[4,18,2048]{2,1,0:T(8,128)}), f32[4,18,2048]{2,1,0:T(8,128)S(1)}, u32[]{:S(2)}, u32[]{:S(2)}) async-start(f32[4,18,2048]{2,1,0:T(8,128)} %reshape.140), calls=%async_computation.1 | async-start | bytes 1572864 | tf_op jit(solution)/shard_map/all_to_all | solution.py:401
  432.1 16.5 %copy-start.2 = (bf16[1024,1152]{1,0:T(8,128)(2,1)S(1)}, bf16[1024,1152]{1,0:T(8,128)(2,1)}, u32[]{:S(2)}) copy-start(bf16[1024,1152]{1,0:T(8,128)(2,1)} %get-tuple-element.9) | copy-start | bytes 7077892
Sparse Core Ops, SparseCore 0:
  22.2 111.1 all-gather.1
  202.3 25.6 all-reduce.1

commit v3 on v2

--- a/solution.py
+++ b/solution.py
@@ -16,6 +16,8 @@
 CHUNKS = 8
 ORDERS = (("x", "y", "z"), ("y", "z", "x"), ("z", "x", "y"))
 STEP = {"x": 1, "y": 4, "z": 16}
+LANE = 128
+ROWS = 256
 F32, BF16 = jnp.float32, jnp.bfloat16
 
 
@@ -26,6 +28,10 @@
 def shifted(me, pos, axis, d):
     there = lax.rem(pos[axis] + d, 4)
     return me + (there - pos[axis]) * STEP[axis]
+
+
+def span(start, size):
+    return pl.ds(pl.multiple_of(start, size), size)
 
 
 def remote(src, dst, send, recv, device):
@@ -40,8 +46,8 @@
 
 
 def grad_kernel(total_tokens, emb_scale, u_ref, table_ref, xt_ref, ids_ref, stat_ref, h_ref, gain_ref, loss_ref,
-                grad_ref, dh_ref, small_ref, own, buf2, buf3, ra0, ra1, ra2, rb, rc, ubuf, tbuf, dz, dxn, dxn_in, sums, sums_in,
-                load_sem, ssem, rsem, xsend, xrecv, sum_send, sum_recv, credit):
+                grad_ref, dh_ref, small_ref, look_ref, own, buf2, buf3, ra0, ra1, ra2, rb, rc, ubuf, tbuf, dz, dxn, dxn_in, look_in, sums, sums_in,
+                load_sem, ssem, rsem, xsend, xrecv, sum_send, sum_recv, credit, look_free):
     me = lax.axis_index("fsdp")
     tp = lax.axis_index("tp")
     pos = coords(me)
@@ -59,7 +65,7 @@
     def loads(i):
         c, q = lax.div(i, NX), lax.rem(i, NX)
         s = lax.rem(i, 2)
-        at = pl.ds(pl.multiple_of(q * quarter + c * lanes, 128), lanes)
+        at = pl.ds(pl.multiple_of(q * quarter + c * lanes, LANE), lanes)
         return (pltpu.make_async_copy(u_ref.at[:, at], ubuf.at[s], load_sem.at[s, 0]),
                 pltpu.make_async_copy(table_ref.at[:, at], tbuf.at[s], load_sem.at[s, 1]))
 
@@ -78,19 +84,22 @@
             first_id = q * quarter + c * lanes
 
             def block(b, carry):
-                r = pl.ds(pl.multiple_of(b * 256, 256), 256)
-                ids = lax.broadcasted_iota(jnp.int32, (256, lanes), 1) + first_id
+                r = span(b * ROWS, ROWS)
+                ids = lax.broadcasted_iota(jnp.int32, (ROWS, lanes), 1) + first_id
                 u = ubuf[s, r]
                 prob = jnp.exp(SOFT_CAP * u - stat_ref[r, 0:1])
                 hit = (ids_ref[r, 1:2] == ids).astype(F32)
                 d = ((prob - hit) * (1.0 - u * u) / total_tokens).astype(BF16)
                 dz[r] = d
-                dz[pl.ds(pl.multiple_of(tokens + b * 256, 256), 256)] = jnp.where(ids_ref[r, 0:1] == ids, emb_scale, 0.0).astype(BF16)
+                pick = jnp.where(ids_ref[r, 0:1] == ids, emb_scale, 0.0).astype(BF16)
+                dz[pl.ds(pl.multiple_of(tokens + b * ROWS, ROWS), ROWS)] = pick
                 part = lax.dot_general(d, tbuf[s], (((1,), (1,)), ((), ())), preferred_element_type=F32)
                 dxn[r] = dxn[r] + part
+                found = lax.dot_general(pick, tbuf[s], (((1,), (1,)), ((), ())), preferred_element_type=F32)
+                look_ref[r] = look_ref[r] + found.astype(BF16)
                 return carry
 
-            lax.fori_loop(0, tokens // 256, block, 0)
+            lax.fori_loop(0, tokens // ROWS, block, 0, unroll=True)
 
             def out(z, carry):
                 w = width // 4
@@ -98,7 +107,7 @@
                 own[slot, q, z] = v.reshape(4, COLORS, rows, lanes)
                 return carry
 
-            lax.fori_loop(0, 4, out, 0)
+            lax.fori_loop(0, 4, out, 0, unroll=True)
             return carry
 
         lax.fori_loop(0, NX, one, 0)
@@ -113,7 +122,7 @@
             return own_at(s, k, a, half)
         if phase == 1:
             return buf2.at[s, k, a, pl.ds(2 * half, 2)]
-        return buf3.at[s, k, a, :, pl.ds(128 * half, 128)]
+        return buf3.at[s, k, a, :, pl.ds(LANE * half, LANE)]
 
     def land(phase, k, s, m):
         return ra[k].at[s, m] if phase == 0 else (rb, rc)[phase - 1].at[s, k, m]
@@ -176,7 +185,7 @@
 
     def store3(c):
         def put(k, half, v):
-            grad_ref[k, :, pl.ds(pl.multiple_of(c * lanes + 128 * half, 128), 128)] = v
+            grad_ref[k, :, pl.ds(pl.multiple_of(c * lanes + LANE * half, LANE), LANE)] = v
         return put
 
     half_rows = tokens // 2
@@ -188,6 +197,16 @@
 
     def swap_dh():
         return remote(dh_ref.at[mine], dh_ref.at[mine], xsend.at[1], xrecv.at[1], partner)
+
+    def swap_look(back):
+        if back:
+            return remote(look_ref.at[mine], look_ref.at[mine], xsend.at[3], xrecv.at[3], partner)
+        return remote(look_ref.at[other], look_in, xsend.at[2], xrecv.at[2], partner)
+
+    def finish_look():
+        swap_look(False).wait()
+        pl.semaphore_signal(look_free, inc=1, device_id=partner, device_id_type=MESH)
+        look_ref[mine] = look_ref[mine] + look_in[...]
 
     def finish_hidden():
         swap_dxn().wait()
@@ -195,8 +214,8 @@
         gain = gain_ref[...]
 
         def block(b, acc):
-            lo = pl.ds(pl.multiple_of(b * 128, 128), 128)
-            r = pl.ds(pl.multiple_of(tp * half_rows + b * 128, 128), 128)
+            lo = span(b * LANE, LANE)
+            r = span(tp * half_rows + b * LANE, LANE)
             inv = stat_ref[r, 1:2]
             hn = h_ref[r].astype(F32) * inv
             dx = dxn[r] + dxn_in[lo]
@@ -205,10 +224,10 @@
             dh_ref[r] = (inv * (g_dir - hn * mean)).astype(BF16)
             return acc + jnp.sum(dx * hn, axis=0, keepdims=True)
 
-        dg = lax.fori_loop(0, half_rows // 128, block, jnp.zeros((1, width), F32))
-        n = width // 128
+        dg = lax.fori_loop(0, half_rows // LANE, block, jnp.zeros((1, width), F32))
+        n = width // LANE
         for i in range(n):
-            sums[pl.ds(i, 1), :] = dg[:, 128 * i:128 * i + 128]
+            sums[pl.ds(i, 1), :] = dg[:, LANE * i:LANE * i + LANE]
         sums[pl.ds(n, 1), :] = loss_ref[...]
         swap_dh().start()
 
@@ -233,6 +252,7 @@
             sums[...] = sums[...] + sums_in[phase, 0] + sums_in[phase, 1] + sums_in[phase, 2]
 
     dxn[...] = jnp.zeros_like(dxn)
+    look_ref[...] = jnp.zeros_like(look_ref)
     for cp in loads(0):
         cp.start()
     ticks = chunks + 6
@@ -265,6 +285,7 @@
         @pl.when(t == chunks - 1)
         def _():
             swap_dxn().start()
+            swap_look(False).start()
         stage(6, lambda c, s: last(2, s, store3(c)))
         stage(5, lambda c, s: second(2, s))
         stage(4, s4)
@@ -279,9 +300,15 @@
         def _():
             sum_start(0)
             swap_dh().wait()
+            finish_look()
         for phase in range(3):
             @pl.when(t == chunks + 2 + phase)
             def _():
+                if phase == 0:
+                    pl.semaphore_wait(look_free, 1)
+                    swap_look(True).start()
+                if phase == 2:
+                    swap_look(True).wait()
                 sum_end(phase)
                 sum_start(phase + 1)
         @pl.when(t == chunks + 5)
@@ -308,9 +335,9 @@
     dma = pltpu.SemaphoreType.DMA
     return pl.pallas_call(
         functools.partial(grad_kernel, total_tokens, emb_scale),
-        out_shape=[jax.ShapeDtypeStruct((COLORS, rows, quarter), F32), jax.ShapeDtypeStruct((tokens, width), BF16), jax.ShapeDtypeStruct((16, 128), F32)],
+        out_shape=[jax.ShapeDtypeStruct((COLORS, rows, quarter), F32), jax.ShapeDtypeStruct((tokens, width), BF16), jax.ShapeDtypeStruct((16, LANE), F32), jax.ShapeDtypeStruct((tokens, width), BF16)],
         in_specs=[hbm, hbm] + [vm] * 6,
-        out_specs=[vm, vm, vm],
+        out_specs=[vm, vm, vm, vm],
         scratch_shapes=[
             pltpu.VMEM((SLOTS, 4, 4, 4, COLORS, rows, lanes), F32),
             pltpu.VMEM((SLOTS, COLORS, 4, 4, rows, lanes), F32),
@@ -319,27 +346,292 @@
             pltpu.VMEM((SLOTS, 6, 4, 2, rows, lanes), F32),
             pltpu.VMEM((SLOTS, 6, 2, 4, rows, lanes), F32),
             pltpu.VMEM((SLOTS, COLORS, 6, 2, rows, lanes), F32),
-            pltpu.VMEM((SLOTS, COLORS, 6, rows, 128), F32),
+            pltpu.VMEM((SLOTS, COLORS, 6, rows, LANE), F32),
             pltpu.VMEM((2, tokens, lanes), F32),
             pltpu.VMEM((2, width, lanes), BF16),
             pltpu.VMEM((2 * tokens, lanes), BF16),
             pltpu.VMEM((tokens, width), F32),
             pltpu.VMEM((tokens // 2, width), F32),
-            pltpu.VMEM((16, 128), F32),
-            pltpu.VMEM((4, 3, 16, 128), F32),
+            pltpu.VMEM((tokens // 2, width), BF16),
+            pltpu.VMEM((16, LANE), F32),
+            pltpu.VMEM((4, 3, 16, LANE), F32),
             dma((2, 2)),
             dma((3, SLOTS, COLORS, 6)),
             dma((3, SLOTS, COLORS, 6)),
-            dma((2,)),
-            dma((2,)),
+            dma((4,)),
+            dma((4,)),
             dma((4, 3)),
             dma((4, 3)),
             pltpu.SemaphoreType.REGULAR((6,)),
+            pltpu.SemaphoreType.REGULAR,
         ],
         compiler_params=pltpu.CompilerParams(collective_id=2, has_side_effects=True, vmem_limit_bytes=63 * 2**20),
     )(u, table, xt, ids, stat, h, gain, loss)
 
 
+def table_kernel(emb_ref, norm_ref, h_ref, g_ref, ids_ref, u_ref, table_ref, xt_ref, stat_ref, gain_ref, loss_ref,
+                 xin, mid, yin, tab, norms, norms_in, xn, rhs, ubuf, acc, sums, sums_in,
+                 ex_send, ex_recv, nsend, nrecv, ssem, rsem, psend, precv, usem, tsem):
+    me = lax.axis_index("fsdp")
+    tp = lax.axis_index("tp")
+    pos = coords(me)
+    tokens, width = h_ref.shape
+    parts, block, lanes = tab.shape[0], tab.shape[5], tab.shape[6]
+    quarter = emb_ref.shape[2]
+    cols = emb_ref.shape[1]
+    sub = quarter // 4
+    peers = {a: [{"fsdp": shifted(me, pos, a, d)} for d in (1, 2, 3)] for a in "xyz"}
+    partner = {"tp": 1 - tp}
+    greet(peers["x"] + peers["y"] + peers["z"] + [partner])
+
+    def exchange(j):
+        axis = "xy"[j]
+        out = []
+        for d in (1, 2, 3):
+            there = lax.rem(pos[axis] + d, 4)
+            src, dst = (emb_ref.at[there], xin.at[pos[axis]]) if j == 0 else (mid.at[there], yin.at[pos[axis]])
+            out.append(remote(src, dst, ex_send.at[j, d - 1], ex_recv.at[j, d - 1], peers[axis][d - 1]))
+        return out
+
+    def norm_copies(j):
+        return [remote(norms, norms_in.at[j, d], nsend.at[j, d], nrecv.at[j, d], peers["xyz"[j]][d]) for d in range(3)]
+
+    def norm_start(j):
+        for cp in norm_copies(j):
+            cp.start()
+
+    def norm_end(j):
+        for cp in norm_copies(j):
+            cp.wait()
+        norms[...] = norms[...] + norms_in[j, 0] + norms_in[j, 1] + norms_in[j, 2]
+
+    norms[...] = norm_ref[...]
+    for cp in exchange(0):
+        cp.start()
+    xin[pos["x"]] = emb_ref[pos["x"]]
+    norm_start(0)
+    for cp in exchange(0):
+        cp.wait()
+    for j in range(4):
+        for i in range(4):
+            mid[j, pl.ds(cols * i, cols), :] = xin[i, :, pl.ds(sub * j, sub)]
+    norm_end(0)
+    norm_start(1)
+    for cp in exchange(1):
+        cp.start()
+    yin[pos["y"]] = mid[pos["y"]]
+    for cp in exchange(1):
+        cp.wait()
+    whole = jnp.concatenate([yin[i] for i in range(4)], axis=0).astype(BF16)
+    for c in range(parts):
+        for k in range(COLORS):
+            tab[c, pos["x"], pos["y"], pos["z"], k] = whole[block * k:block * k + block, lanes * c:lanes * c + lanes]
+    norm_end(1)
+    norm_start(2)
+
+    def region(e, kind, k, a, half):
+        o = ORDERS[k]
+        if kind == 0:
+            sel = {o[0]: pos[o[0]], o[1]: pos[o[1]], o[2]: a}
+            return tab.at[:, sel["x"], sel["y"], sel["z"], k, pl.ds(half * (block // 2), block // 2)]
+        if kind == 1:
+            sel = {o[0]: pos[o[0]], o[1]: a, o[2]: pl.ds(2 * half, 2)}
+            return tab.at[:, sel["x"], sel["y"], sel["z"], k]
+        sel = {o[0]: a, o[1]: pl.ds(2 * half, 2), o[2]: slice(None)}
+        return tab.at[e - 2, sel["x"], sel["y"], sel["z"], k]
+
+    def copies(e, k, step):
+        kind = min(e, 2) if isinstance(e, int) else 2
+        axis = ORDERS[k][2 - kind]
+        p = pos[axis]
+        right, left = lax.rem(p + 1, 4), lax.rem(p + 3, 4)
+        to_r, to_l = {"fsdp": shifted(me, pos, axis, 1)}, {"fsdp": shifted(me, pos, axis, 3)}
+        if step == 0:
+            plan = ((0, p, 0, to_r), (1, p, 1, to_l), (2, p, 1, to_r), (3, p, 0, to_l))
+        else:
+            plan = ((4, left, 0, to_r), (5, right, 1, to_l))
+        return [remote(region(e, kind, k, a, half), region(e, kind, k, a, half), ssem.at[e, k, m], rsem.at[e, k, m], dev)
+                for m, a, half, dev in plan]
+
+    def begin(e):
+        for k in range(COLORS):
+            for cp in copies(e, k, 0):
+                cp.start()
+
+    def forward(e):
+        for k in range(COLORS):
+            one, two = copies(e, k, 0), copies(e, k, 1)
+            one[0].wait_recv()
+            two[0].start()
+            one[1].wait_recv()
+            two[1].start()
+
+    def arrive(e):
+        for k in range(COLORS):
+            one, two = copies(e, k, 0), copies(e, k, 1)
+            for cp in one[2:] + two:
+                cp.wait_recv()
+            for cp in one + two:
+                cp.wait_send()
+
+    begin(0)
+    forward(0)
+    arrive(0)
+    begin(1)
+    norm_end(2)
+    n = width // LANE
+    gain = 1.0 + jnp.concatenate([norms[pl.ds(i, 1), :] for i in range(n)], axis=1)
+    gain_ref[...] = gain
+
+    def normalize(b, carry):
+        r = span(b * LANE, LANE)
+        hw = h_ref[r].astype(F32)
+        inv = lax.rsqrt(jnp.mean(hw * hw, axis=1, keepdims=True) + NORM_EPS)
+        v = (hw * inv * gain_ref[...]).astype(BF16)
+        xn[r] = v
+        stat_ref[r, 1:2] = inv
+        xt_ref[:, r] = v.T
+        xt_ref[:, span(tokens + b * LANE, LANE)] = g_ref[r].T
+        return carry
+
+    lax.fori_loop(0, tokens // LANE, normalize, 0)
+    forward(1)
+    acc[...] = jnp.zeros_like(acc)
+    arrive(1)
+    begin(2)
+
+    def u_out(i):
+        c, p = lax.div(i, 8), lax.rem(i, 8)
+        s = lax.rem(i, 2)
+        base = lax.div(p, 2) * quarter + lax.rem(p, 2) * (2 * sub) + c * lanes
+        return [pltpu.make_async_copy(ubuf.at[s, j], u_ref.at[:, pl.ds(pl.multiple_of(base + j * sub, LANE), lanes)], usem.at[s, j]) for j in range(2)]
+
+    def table_out(c):
+        cps = []
+        for x in range(4):
+            for y in range(4):
+                at = pl.ds(pl.multiple_of(x * quarter + y * sub + c * lanes, LANE), lanes)
+                cps.append(pltpu.make_async_copy(tab.at[c, x, y], table_ref.at[:, :, :, at], tsem.at[x, y]))
+        return cps
+
+    def chunk(c, carry):
+        forward(c + 2)
+
+        @pl.when(c + 1 < parts)
+        def _():
+            begin(c + 3)
+
+        arrive(c + 2)
+
+        @pl.when(c >= 1)
+        def _():
+            for cp in table_out(c - 1):
+                cp.wait()
+        for cp in table_out(c):
+            cp.start()
+
+        def pair(p, carry):
+            i = c * 8 + p
+            s = lax.rem(i, 2)
+            x, y = lax.div(p, 2), lax.rem(p, 2) * 2
+            for j in range(2):
+                rhs[:, lanes * j:lanes * j + lanes] = tab[c, x, y + j].reshape(width, lanes)
+
+            @pl.when(i >= 2)
+            def _():
+                for cp in u_out(i - 2):
+                    cp.wait()
+            base = x * quarter + y * sub + c * lanes
+            lane = lax.broadcasted_iota(jnp.int32, (ROWS, 2 * lanes), 1)
+            ids = lane + base + jnp.where(lane >= lanes, sub - lanes, 0)
+
+            def rows(b, carry):
+                r = span(b * ROWS, ROWS)
+                z = jnp.dot(xn[r], rhs[...], preferred_element_type=F32)
+                u = jnp.tanh(z * (1.0 / SOFT_CAP))
+                for j in range(2):
+                    ubuf[s, j, r] = u[:, lanes * j:lanes * j + lanes]
+                capped = SOFT_CAP * u
+                e = jnp.exp(capped - SOFT_CAP)
+                hit = jnp.where(ids_ref[r, 1:2] == ids, capped, 0.0)
+                acc[0, r] = acc[0, r] + e[:, :lanes] + e[:, lanes:]
+                acc[1, r] = acc[1, r] + hit[:, :lanes] + hit[:, lanes:]
+                return carry
+
+            lax.fori_loop(0, tokens // ROWS, rows, 0, unroll=True)
+            for cp in u_out(i):
+                cp.start()
+            return carry
+
+        lax.fori_loop(0, 8, pair, 0)
+        return carry
+
+    lax.fori_loop(0, parts, chunk, 0)
+    lane = lax.broadcasted_iota(jnp.int32, (tokens, LANE), 1)
+    sums[...] = jnp.where(lane == 0, jnp.sum(acc[0], axis=1, keepdims=True), jnp.sum(acc[1], axis=1, keepdims=True))
+    swap = remote(sums, sums_in, psend, precv, partner)
+    swap.start()
+    for cp in u_out(parts * 8 - 2) + u_out(parts * 8 - 1) + table_out(parts - 1):
+        cp.wait()
+    swap.wait()
+    both = sums[...] + sums_in[...]
+    lse = jnp.log(both[:, 0:1]) + SOFT_CAP
+    stat_ref[:, 0:1] = lse
+    loss_ref[...] = jnp.broadcast_to(0.5 * jnp.sum(lse - both[:, 1:2], axis=0, keepdims=True), (1, LANE))
+
+
+def table_pass(emb, norm, h, g, ids):
+    tokens, width = h.shape
+    quarter = emb.shape[2]
+    cols = emb.shape[1]
+    vocab = NX * quarter
+    sub = quarter // 4
+    block = width // 12
+    parts = sub // LANE
+    vm = pl.BlockSpec(memory_space=pltpu.VMEM)
+    hbm = pl.BlockSpec(memory_space=pl.ANY)
+    dma = pltpu.SemaphoreType.DMA
+    u, table, xt, stat, gain, loss = pl.pallas_call(
+        table_kernel,
+        out_shape=[
+            jax.ShapeDtypeStruct((tokens, vocab), F32),
+            jax.ShapeDtypeStruct((4, COLORS, block, vocab), BF16),
+            jax.ShapeDtypeStruct((width, 2 * tokens), BF16),
+            jax.ShapeDtypeStruct((tokens, 2), F32),
+            jax.ShapeDtypeStruct((1, width), F32),
+            jax.ShapeDtypeStruct((1, LANE), F32),
+        ],
+        in_specs=[vm] * 5,
+        out_specs=[hbm, hbm, vm, vm, vm, vm],
+        scratch_shapes=[
+            pltpu.VMEM((4, cols, quarter), F32),
+            pltpu.VMEM((4, 4 * cols, sub), F32),
+            pltpu.VMEM((4, 4 * cols, sub), F32),
+            pltpu.VMEM((parts, 4, 4, 4, COLORS, block, LANE), BF16),
+            pltpu.VMEM((16, LANE), F32),
+            pltpu.VMEM((3, 3, 16, LANE), F32),
+            pltpu.VMEM((tokens, width), BF16),
+            pltpu.VMEM((width, ROWS), BF16),
+            pltpu.VMEM((2, 2, tokens, LANE), F32),
+            pltpu.VMEM((2, tokens, LANE), F32),
+            pltpu.VMEM((tokens, LANE), F32),
+            pltpu.VMEM((tokens, LANE), F32),
+            dma((2, 3)),
+            dma((2, 3)),
+            dma((3, 3)),
+            dma((3, 3)),
+            dma((2 + parts, COLORS, 6)),
+            dma((2 + parts, COLORS, 6)),
+            dma,
+            dma,
+            dma((2, 2)),
+            dma((4, 4)),
+        ],
+        compiler_params=pltpu.CompilerParams(collective_id=1, has_side_effects=True, vmem_limit_bytes=63 * 2**20),
+    )(emb, norm, h, g, ids)
+    return u, table.reshape(width, vocab), xt, stat, gain, loss
+
+
 def math_scale(width):
     import numpy as np
     return float(np.asarray(math.sqrt(width), BF16).astype(np.float32))
@@ -347,8 +639,7 @@
 
 def solution(mesh):
     fsdp_size = mesh.shape["fsdp"]
-    groups = fsdp_size // NX
-    x_groups = [[i * NX + j for j in range(NX)] for i in range(groups)]
+    x_groups = [[i * NX + j for j in range(NX)] for i in range(fsdp_size // NX)]
 
     def device_step(emb_shard, tok_ids, lab_ids, h_last, g_embed, norm_w):
         vocab_rows, cols = emb_shard.shape
@@ -358,45 +649,15 @@
         quarter = vocab_rows // NX
         row_start = lax.axis_index("tp") * vocab_rows
         me = lax.axis_index("fsdp")
-        vocab_iota = jnp.arange(vocab_rows, dtype=jnp.int32)
-        emb_scale = jnp.asarray(math.sqrt(width), jnp.bfloat16).astype(jnp.float32)
-
-        piece = emb_shard.T.astype(jnp.bfloat16).reshape(cols, NX, quarter).transpose(1, 0, 2)
-        piece = lax.all_to_all(piece, "fsdp", split_axis=0, concat_axis=0, axis_index_groups=x_groups)
-        piece = piece.reshape(NX * cols, quarter)
-        table = lax.all_gather(piece, "fsdp", axis=0)
-        table = table.reshape(groups, NX, NX * cols, quarter).transpose(0, 2, 1, 3).reshape(width, vocab_rows)
-
-        tok_local = tok_ids.reshape(tok_count) - row_start
-        tok_hit = (tok_local[:, None] == vocab_iota[None, :]).astype(jnp.bfloat16)
-        row_vals = jnp.einsum("tv,dv->td", tok_hit, table, preferred_element_type=jnp.float32).astype(jnp.bfloat16)
-        row_vals = lax.psum(row_vals, "tp")
-        x_emb = (row_vals.astype(jnp.float32) * emb_scale).astype(jnp.bfloat16)
-
-        mine = jnp.where(lax.axis_index("tp") == 0, norm_w, 0.0)
-        norm_full = lax.dynamic_update_slice(jnp.zeros((width,), jnp.float32), mine, (me * cols,))
-        norm_gain = 1.0 + lax.psum(norm_full, ("tp", "fsdp"))
-        h_wide = h_last.reshape(tok_count, width).astype(jnp.float32)
-        inv_rms = lax.rsqrt(jnp.mean(h_wide * h_wide, axis=1, keepdims=True) + NORM_EPS)
-        h_norm = h_wide * inv_rms
-        x_norm = (h_norm * norm_gain).astype(jnp.bfloat16)
-
-        logits = jnp.einsum("td,dv->tv", x_norm, table, preferred_element_type=jnp.float32)
-        tanh_z = jnp.tanh(logits / SOFT_CAP)
-        capped = SOFT_CAP * tanh_z
-        exp_shift = jnp.exp(capped - SOFT_CAP)
-        lab_hit = (lab_ids.reshape(tok_count) - row_start)[:, None] == vocab_iota[None, :]
-        tok_stats = jnp.stack([jnp.sum(exp_shift, axis=1), jnp.sum(jnp.where(lab_hit, capped, 0.0), axis=1)])
-        tok_stats = lax.psum(tok_stats, "tp")
-        sum_exp = tok_stats[0]
-        log_norm = jnp.log(sum_exp) + SOFT_CAP
-        loss_part = 0.5 * jnp.sum(log_norm - tok_stats[1])
-
-        xt = jnp.concatenate([x_norm.T, g_embed.reshape(tok_count, width).T], axis=1)
-        ids = jnp.stack([tok_local, lab_ids.reshape(tok_count) - row_start], axis=1)
-        stat = jnp.concatenate([log_norm[:, None], inv_rms], axis=1)
-        grad, d_hidden, small = gradients(total_tokens, math_scale(width), tanh_z, table, xt, ids, stat, h_last.reshape(tok_count, width), norm_gain[None, :], jnp.full((1, 128), loss_part))
-        loss_val = small[width // 128, 0] / total_tokens
+
+        emb = emb_shard.T.reshape(cols, NX, quarter).transpose(1, 0, 2)
+        norm = lax.dynamic_update_slice(jnp.zeros((16 * LANE,), F32), norm_w, (me * cols,)).reshape(16, LANE)
+        ids = jnp.stack([tok_ids.reshape(tok_count) - row_start, lab_ids.reshape(tok_count) - row_start], axis=1)
+        h = h_last.reshape(tok_count, width)
+        g = g_embed.reshape(tok_count, width)
+        u, table, xt, stat, gain, loss = table_pass(emb, norm, h, g, ids)
+        grad, d_hidden, small, x_emb = gradients(total_tokens, math_scale(width), u, table, xt, ids, stat, h, gain, loss)
+        loss_val = small[width // LANE, 0] / total_tokens
         d_norm_w = lax.dynamic_slice(small.reshape(-1), (me * cols,), (cols,))
         grad = lax.all_to_all(grad.reshape(NX, cols, quarter), "fsdp", split_axis=0, concat_axis=0, axis_index_groups=x_groups)
         d_table = grad.transpose(1, 0, 2).reshape(cols, vocab_rows).T

time: 459 us -> 329 us (0.72)
  Pallas kernels: 182 us -> 299 us
  blocking collectives: 82.1 us -> 0 us
  matrix products: 68.1 us -> 0 us
  local copies, waits for them, and re-layouts: 56.1 us -> 15 us
  waiting for transfers between devices: 39.3 us -> 7.85 us
  between operations: 16.6 us -> 2.49 us
  other arithmetic: 9.93 us -> 0.72 us
    pallas_call x0 -> x1, Pallas kernels: none -> 127 us  [table_pass(): pl.pallas_call(table_kernel, out_shape=[jax.ShapeDtypeStruct((tokens, voc...]
    psum x2 -> x0, blocking collectives: 69.7 us -> none  [the longest x1 67 us: device_step(): norm_gain = 1.0 + lax.psum(norm_full, ('tp', 'fsdp'))]
    dot_general x2 -> x0, matrix products: 68.1 us -> none  [the longest x1 36.5 us: device_step(): jnp.einsum('td,dv->tv', x_norm, table, preferred_element_type=jnp.float32)]
    all_gather x1 -> x0, waiting for transfers between devices: 31.4 us -> none  [device_step(): table = lax.all_gather(piece, 'fsdp', axis=0)]
    transpose x1 -> x0, local copies, waits for them, and re-layouts: 21.3 us -> none  [device_step(): table.reshape(groups, NX, NX * cols, quarter).transpose(0, 2, 1, 3)]
    unnamed x16 -> x12, local copies, waits for them, and re-layouts: 18.8 us -> 6.04 us
    all_to_all x1 -> x0, blocking collectives: 12.3 us -> none  [device_step(): lax.all_to_all(piece, 'fsdp', split_axis=0, concat_axis=0, axis_index_gro...]
    pallas_call x1, Pallas kernels: 182 us -> 172 us  [gradients(): pl.pallas_call(functools.partial(grad_kernel, total_tokens, emb_scale), o...]
  transfers between devices with their start and end apart: 3 -> 1, of which waited for: 2 -> 1; matrix products, arithmetic and copies ran while one was open for 13% -> 1% of each run, Pallas kernels for 40% -> 0%
where the time goes in v3:
time: 329 us; the launch traced here: 328 us
  Pallas kernels  299 us (91%)
  local copies, waits for them, and re-layouts  15 us (5%)
  waiting for transfers between devices  7.85 us (2%)
  starting transfers between devices  3.49 us (1%)
    pallas_call x1, Pallas kernels, gradients(): pl.pallas_call(functools.partial(grad_kernel, total_tokens, emb_scale), o...  172 us
    pallas_call x1, Pallas kernels, table_pass(): pl.pallas_call(table_kernel, out_shape=[jax.ShapeDtypeStruct((tokens, voc...  127 us
    all_to_all x1, waiting for transfers between devices, device_step(): lax.all_to_all(grad.reshape(NX, cols, quarter), 'fsdp', split_axis=0, con...  7.85 us
  transfers between devices with their start and end apart: 1, of which 1 were waited for; matrix products, arithmetic and copies ran while one was open for 1% of the time, Pallas kernels for 0%

profile of v3, /device:TPU:0, one launch (start us, length us, event | category | flops | bytes accessed | tf_op | source)
XLA Modules:
  0.0 328.5 jit_solution(9367392828632677359)
XLA Ops:
  0.6 0.0 copy-start.3
  0.6 0.7 subtract_bitcast_fusion
  1.4 1.0 copy.20.ids_ref
  2.4 1.5 reshape.68
  3.9 1.2 copy.25
  5.2 0.0 copy-done.3
  5.2 0.2 dynamic_update_slice.3
  5.4 0.0 copy-start.2
  5.4 0.6 copy-done.2
  6.0 127.3 %shard_map.101 = (f32[1024,8192]{1,0:T(8,128)}, bf16[4,3,96,8192]{3,2,1,0:T(8,128)(2,1)}, bf16[1152,2048]{1,0:T(8,128)(2,1)}, f32[1024,2]{1,0:T(8,128)}, f32[1,1152]{1,0:T(1,128)}, /*index=5*/f32[1,128]{1,0:T(1,128)}) custom-call(f32[4,18,2048]{2,1,0:T(8,128)} %bitcast.27, f32[16,128]{1,0:T(8,128)} %bitcast.33, bf16[1024,1152]{1,0:T(8,128)(2,1)} %bitcast.23, ...), custom_call_target="tpu_custom_call" | custom-call | tf_op jit(solution)/shard_map/pallas_call | solution.py:594
  133.3 171.5 %shard_map.102 = (f32[3,24,2048]{2,1,0:T(8,128)}, bf16[1024,1152]{1,0:T(8,128)(2,1)}, f32[16,128]{1,0:T(8,128)}, bf16[1024,1152]{1,0:T(8,128)(2,1)}) custom-call(f32[1024,8192]{1,0:T(8,128)} %get-tuple-element.15.u_ref, bf16[1152,8192]{1,0:T(8,128)(2,1)} %bitcast.22, bf16[1152,2048]{1,0:T(8,128)(2,1)} %get-tuple-element.17.xt_ref, s32[1024,2]{1,0:T(8,128)} %copy.20.ids_ref, ...), custom_call_target="tpu_custom_call" | custom-call | tf_op jit(solution)/shard_map/pallas_call | solution.py:336
  304.8 2.0 reshape.76
  306.9 3.5 %all-to-all-start = ((f32[4,18,2048]{2,1,0:T(8,128)}), f32[4,18,2048]{2,1,0:T(8,128)S(1)}, u32[]{:S(2)}, u32[]{:S(2)}) async-start(f32[4,18,2048]{2,1,0:T(8,128)} %reshape.76), calls=%async_computation | async-start | bytes 1572864 | tf_op jit(solution)/shard_map/all_to_all | solution.py:662
  310.4 0.0 copy-start.1
  310.4 1.3 slice.3
  311.7 1.3 dynamic_slice.3
  313.6 7.9 %all-to-all-done = f32[4,18,2048]{2,1,0:T(8,128)S(1)} async-done(((f32[4,18,2048]{2,1,0:T(8,128)}), f32[4,18,2048]{2,1,0:T(8,128)S(1)}, u32[]{:S(2)}, u32[]{:S(2)}) %all-to-all-start) | async-done | bytes 589856 | tf_op jit(solution)/shard_map/all_to_all | solution.py:662
  321.5 0.4 copy.22
  321.9 0.2 pad.2
  322.1 1.3 copy.23
  323.4 0.0 copy-done.1
  323.4 0.0 copy-start
  323.4 1.4 copy.29
  324.8 1.1 copy-done
  325.9 1.4 copy.30
  (2 shorter events, 0.0 us)
Async XLA Ops:
  0.6 4.5 %copy-start.3 = (f32[18]{0:T(128)S(1)}, f32[18]{0:T(128)}, u32[]{:S(2)}) copy-start(f32[18]{0:T(128)} %param.11) | copy-start | bytes 220
  5.4 0.6 copy-start.2
  306.9 14.6 %all-to-all-start = ((f32[4,18,2048]{2,1,0:T(8,128)}), f32[4,18,2048]{2,1,0:T(8,128)S(1)}, u32[]{:S(2)}, u32[]{:S(2)}) async-start(f32[4,18,2048]{2,1,0:T(8,128)} %reshape.76), calls=%async_computation | async-start | bytes 1572864 | tf_op jit(solution)/shard_map/all_to_all | solution.py:662
  310.4 13.0 %copy-start.1 = (bf16[1024,1152]{1,0:T(8,128)(2,1)S(1)}, bf16[1024,1152]{1,0:T(8,128)(2,1)}, u32[]{:S(2)}) copy-start(bf16[1024,1152]{1,0:T(8,128)(2,1)} %get-tuple-element.21) | copy-start | bytes 7077892
  323.4 2.5 copy-start

commit v4 on v3

--- a/solution.py
+++ b/solution.py
@@ -41,13 +41,13 @@
 def greet(devices):
     barrier = pltpu.get_barrier_semaphore()
     for n in devices:
-        pl.semaphore_signal(barrier, inc=1, device_id=n, device_id_type=MESH)
+        pl.semaphore_signal(barrier, device_id=n, device_id_type=MESH)
     pl.semaphore_wait(barrier, len(devices))
 
 
 def grad_kernel(total_tokens, emb_scale, u_ref, table_ref, xt_ref, ids_ref, stat_ref, h_ref, gain_ref, loss_ref,
-                grad_ref, dh_ref, small_ref, look_ref, own, buf2, buf3, ra0, ra1, ra2, rb, rc, ubuf, tbuf, dz, dxn, dxn_in, look_in, sums, sums_in,
-                load_sem, ssem, rsem, xsend, xrecv, sum_send, sum_recv, credit, look_free):
+                grad_ref, dh_ref, small_ref, look_ref, own, buf2, buf3, ra0, ra1, ra2, rb, rc, ubuf, tbuf, dz, dxn, dxn_in, look_in, piece, sums, sums_in,
+                load_sem, ssem, rsem, xsend, xrecv, sum_send, sum_recv, psend, precv, credit, look_free):
     me = lax.axis_index("fsdp")
     tp = lax.axis_index("tp")
     pos = coords(me)
@@ -56,11 +56,15 @@
     rows = own.shape[-2]
     tokens, width = h_ref.shape
     vocab = u_ref.shape[1]
+    cols = grad_ref.shape[0]
     quarter = vocab // NX
     ra = (ra0, ra1, ra2)
     near = [{"fsdp": shifted(me, pos, a, d)} for a in "xyz" for d in (1, 3)]
     partner = {"tp": 1 - tp}
-    greet(near + [{"fsdp": shifted(me, pos, a, 2)} for a in "xyz"] + [partner])
+    everyone = near + [{"fsdp": shifted(me, pos, a, 2)} for a in "xyz"] + [partner]
+    barrier = pltpu.get_barrier_semaphore()
+    for n in everyone:
+        pl.semaphore_signal(barrier, device_id=n, device_id_type=MESH)
 
     def loads(i):
         c, q = lax.div(i, NX), lax.rem(i, NX)
@@ -89,7 +93,7 @@
                 u = ubuf[s, r]
                 prob = jnp.exp(SOFT_CAP * u - stat_ref[r, 0:1])
                 hit = (ids_ref[r, 1:2] == ids).astype(F32)
-                d = ((prob - hit) * (1.0 - u * u) / total_tokens).astype(BF16)
+                d = ((prob - hit) * (1.0 - u * u) * (1.0 / total_tokens)).astype(BF16)
                 dz[r] = d
                 pick = jnp.where(ids_ref[r, 0:1] == ids, emb_scale, 0.0).astype(BF16)
                 dz[pl.ds(pl.multiple_of(tokens + b * ROWS, ROWS), ROWS)] = pick
@@ -102,69 +106,76 @@
             lax.fori_loop(0, tokens // ROWS, block, 0, unroll=True)
 
             def out(z, carry):
-                w = width // 4
+                w = width // 2
                 v = jnp.dot(xt_ref[pl.ds(pl.multiple_of(z * w, 32), w), :], dz[...], preferred_element_type=F32)
-                own[slot, q, z] = v.reshape(4, COLORS, rows, lanes)
+                own[slot, q, pl.ds(2 * z, 2)] = v.reshape(2, 4, COLORS, rows, lanes)
                 return carry
 
-            lax.fori_loop(0, 4, out, 0, unroll=True)
+            lax.fori_loop(0, 2, out, 0, unroll=True)
             return carry
 
         lax.fori_loop(0, NX, one, 0)
 
-    def own_at(s, k, a1, half):
+    def own_at(c, k, a1, half):
         o = ORDERS[k]
         sel = {o[0]: a1, o[1]: pl.ds(2 * half, 2), o[2]: slice(None)}
-        return own.at[s, sel["x"], sel["z"], sel["y"], k]
-
-    def part(phase, k, s, a, half):
+        return own.at[lax.rem(c, SLOTS), sel["x"], sel["z"], sel["y"], k]
+
+    def split(half):
+        return pl.ds(16 * half, 16 - 8 * half)
+
+    def part(phase, k, c, a, half):
+        s = lax.rem(c, SLOTS)
         if phase == 0:
-            return own_at(s, k, a, half)
+            return own_at(c, k, a, half)
         if phase == 1:
             return buf2.at[s, k, a, pl.ds(2 * half, 2)]
-        return buf3.at[s, k, a, :, pl.ds(LANE * half, LANE)]
-
-    def land(phase, k, s, m):
-        return ra[k].at[s, m] if phase == 0 else (rb, rc)[phase - 1].at[s, k, m]
-
-    def copies(phase, k, s, step):
+        return buf3.at[s, k, a, split(half)]
+
+    def land(phase, k, c, m):
+        s = lax.rem(c, SLOTS)
+        if phase == 0:
+            return ra[k].at[s, m]
+        return rb.at[s, k, m] if phase == 1 else rc.at[s, k, m, pl.ds(0, 8 if m in (1, 2, 5) else 16)]
+
+    def copies(phase, k, c, step):
         axis = ORDERS[k][phase]
         p = pos[axis]
         right, left, far = lax.rem(p + 1, 4), lax.rem(p + 3, 4), lax.rem(p + 2, 4)
         to_r, to_l = {"fsdp": shifted(me, pos, axis, 1)}, {"fsdp": shifted(me, pos, axis, 3)}
         if step == 0:
-            table = ((0, part(phase, k, s, far, 0), to_r), (1, part(phase, k, s, far, 1), to_l),
-                     (2, part(phase, k, s, right, 1), to_r), (3, part(phase, k, s, left, 0), to_l))
+            table = ((0, part(phase, k, c, far, 0), to_r), (1, part(phase, k, c, far, 1), to_l),
+                     (2, part(phase, k, c, right, 1), to_r), (3, part(phase, k, c, left, 0), to_l))
         else:
-            table = ((4, land(phase, k, s, 0), to_r), (5, land(phase, k, s, 1), to_l))
-        return [(m, remote(src, land(phase, k, s, m), ssem.at[phase, s, k, m], rsem.at[phase, s, k, m], dev)) for m, src, dev in table]
-
-    def first(phase, s):
+            table = ((4, land(phase, k, c, 0), to_r), (5, land(phase, k, c, 1), to_l))
+        return [(m, remote(src, land(phase, k, c, m), ssem.at[phase, lax.rem(c, SLOTS), k, m], rsem.at[phase, lax.rem(c, SLOTS), k, m], dev)) for m, src, dev in table]
+
+    def first(phase, c):
         for k in range(COLORS):
-            for _, cp in copies(phase, k, s, 0):
+            for _, cp in copies(phase, k, c, 0):
                 cp.start()
 
-    def second(phase, s):
+    def second(phase, c):
         for k in range(COLORS):
             axis = ORDERS[k][phase]
             p = pos[axis]
             right, left = lax.rem(p + 1, 4), lax.rem(p + 3, 4)
-            one = copies(phase, k, s, 0)
+            one = copies(phase, k, c, 0)
             for m, a in ((0, right), (1, left)):
                 one[m][1].wait_recv()
-                dst = land(phase, k, s, m)
-                dst[...] = dst[...] + part(phase, k, s, a, m)[...]
-            for _, cp in copies(phase, k, s, 1):
+                dst = land(phase, k, c, m)
+                dst[...] = dst[...] + part(phase, k, c, a, m)[...]
+            for _, cp in copies(phase, k, c, 1):
                 cp.start()
 
-    def last(phase, s, store):
+    def last(phase, c, store):
         for k in range(COLORS):
             p = pos[ORDERS[k][phase]]
-            one, two = copies(phase, k, s, 0), copies(phase, k, s, 1)
+            one, two = copies(phase, k, c, 0), copies(phase, k, c, 1)
             for m, cp in one[2:] + two:
                 cp.wait_recv()
             for half, (m, n) in enumerate(((4, 3), (5, 2))):
-                store(k, half, part(phase, k, s, p, half)[...] + land(phase, k, s, m)[...] + land(phase, k, s, n)[...])
+                store(k, half, part(phase, k, c, p, half)[...] + land(phase, k, c, m)[...] + land(phase, k, c, n)[...])
             for m, cp in one + two:
                 cp.wait_send()
 
@@ -184,9 +195,34 @@
         return put
 
     def store3(c):
+        s = lax.rem(c, SLOTS)
+
         def put(k, half, v):
-            grad_ref[k, :, pl.ds(pl.multiple_of(c * lanes + LANE * half, LANE), LANE)] = v
+            low = rows * k + 16 * half
+            size = 16 - 8 * half
+            for x in range(NX):
+                lo, hi = max(low, x * cols), min(low + size, x * cols + cols)
+                if lo < hi:
+                    piece[s, x, lo - x * cols:hi - x * cols] = v[lo - low:hi - low]
         return put
+
+    def home(c, x):
+        return grad_ref.at[:, pl.ds(pl.multiple_of(x * quarter + c * lanes, LANE), lanes)]
+
+    def hand_out(c):
+        p = pos["x"]
+        return [remote(piece.at[lax.rem(c, SLOTS), lax.rem(p + d, NX)], home(c, p), psend.at[c, d - 1], precv.at[c, d - 1],
+                       {"fsdp": shifted(me, pos, "x", d)}) for d in (1, 2, 3)]
+
+    def finish_piece(c):
+        last(2, c, store3(c))
+        home(c, pos["x"])[...] = piece[lax.rem(c, SLOTS), pos["x"]]
+        for cp in hand_out(c):
+            cp.start()
+
+    def collect(c):
+        for cp in hand_out(c):
+            cp.wait()
 
     half_rows = tokens // 2
     mine = pl.ds(pl.multiple_of(tp * half_rows, half_rows), half_rows)
@@ -205,7 +241,7 @@
 
     def finish_look():
         swap_look(False).wait()
-        pl.semaphore_signal(look_free, inc=1, device_id=partner, device_id_type=MESH)
+        pl.semaphore_signal(look_free, device_id=partner, device_id_type=MESH)
         look_ref[mine] = look_ref[mine] + look_in[...]
 
     def finish_hidden():
@@ -255,43 +291,48 @@
     look_ref[...] = jnp.zeros_like(look_ref)
     for cp in loads(0):
         cp.start()
-    ticks = chunks + 6
+    ticks = chunks + 7
 
     def tick(t, carry):
         @pl.when(t < chunks)
         def _():
             produce(t, lax.rem(t, SLOTS))
 
+        @pl.when(t == 0)
+        def _():
+            pl.semaphore_wait(barrier, len(everyone))
+
         @pl.when(t >= 1)
         def _():
             for i in range(6):
-                pl.semaphore_wait(credit.at[i], 1)
+                pl.semaphore_wait(credit.at[i])
 
         def stage(delay, run):
             c = t - delay
             @pl.when(jnp.logical_and(c >= 0, c < chunks))
             def _():
-                run(c, lax.rem(c, SLOTS))
-
-        def s2(c, s):
-            last(0, s, store1(s))
-            first(1, s)
-
-        def s4(c, s):
-            last(1, s, store2(s))
-            first(2, s)
-
-        stage(0, lambda c, s: first(0, s))
+                run(c)
+
+        def s2(c):
+            last(0, c, store1(lax.rem(c, SLOTS)))
+            first(1, c)
+
+        def s4(c):
+            last(1, c, store2(lax.rem(c, SLOTS)))
+            first(2, c)
+
+        stage(0, lambda c: first(0, c))
         @pl.when(t == chunks - 1)
         def _():
             swap_dxn().start()
             swap_look(False).start()
-        stage(6, lambda c, s: last(2, s, store3(c)))
-        stage(5, lambda c, s: second(2, s))
+        stage(7, collect)
+        stage(6, finish_piece)
+        stage(5, lambda c: second(2, c))
         stage(4, s4)
-        stage(3, lambda c, s: second(1, s))
+        stage(3, lambda c: second(1, c))
         stage(2, s2)
-        stage(1, lambda c, s: second(0, s))
+        stage(1, lambda c: second(0, c))
 
         @pl.when(t == chunks)
         def _():
@@ -305,7 +346,7 @@
             @pl.when(t == chunks + 2 + phase)
             def _():
                 if phase == 0:
-                    pl.semaphore_wait(look_free, 1)
+                    pl.semaphore_wait(look_free)
                     swap_look(True).start()
                 if phase == 2:
                     swap_look(True).wait()
@@ -318,7 +359,7 @@
         @pl.when(t < ticks - 1)
         def _():
             for i, n in enumerate(near):
-                pl.semaphore_signal(credit.at[i], inc=1, device_id=n, device_id_type=MESH)
+                pl.semaphore_signal(credit.at[i], device_id=n, device_id_type=MESH)
         return carry
 
     lax.fori_loop(0, ticks, tick, 0)
@@ -335,7 +376,7 @@
     dma = pltpu.SemaphoreType.DMA
     return pl.pallas_call(
         functools.partial(grad_kernel, total_tokens, emb_scale),
-        out_shape=[jax.ShapeDtypeStruct((COLORS, rows, quarter), F32), jax.ShapeDtypeStruct((tokens, width), BF16), jax.ShapeDtypeStruct((16, LANE), F32), jax.ShapeDtypeStruct((tokens, width), BF16)],
+        out_shape=[jax.ShapeDtypeStruct((width // (NX * NX * NX), vocab), F32), jax.ShapeDtypeStruct((tokens, width), BF16), jax.ShapeDtypeStruct((16, LANE), F32), jax.ShapeDtypeStruct((tokens, width), BF16)],
         in_specs=[hbm, hbm] + [vm] * 6,
         out_specs=[vm, vm, vm, vm],
         scratch_shapes=[
@@ -346,13 +387,14 @@
             pltpu.VMEM((SLOTS, 6, 4, 2, rows, lanes), F32),
             pltpu.VMEM((SLOTS, 6, 2, 4, rows, lanes), F32),
             pltpu.VMEM((SLOTS, COLORS, 6, 2, rows, lanes), F32),
-            pltpu.VMEM((SLOTS, COLORS, 6, rows, LANE), F32),
+            pltpu.VMEM((SLOTS, COLORS, 6, 16, lanes), F32),
             pltpu.VMEM((2, tokens, lanes), F32),
             pltpu.VMEM((2, width, lanes), BF16),
             pltpu.VMEM((2 * tokens, lanes), BF16),
             pltpu.VMEM((tokens, width), F32),
             pltpu.VMEM((tokens // 2, width), F32),
             pltpu.VMEM((tokens // 2, width), BF16),
+            pltpu.VMEM((SLOTS, NX, width // (NX * NX * NX), lanes), F32),
             pltpu.VMEM((16, LANE), F32),
             pltpu.VMEM((4, 3, 16, LANE), F32),
             dma((2, 2)),
@@ -362,6 +404,8 @@
             dma((4,)),
             dma((4, 3)),
             dma((4, 3)),
+            dma((CHUNKS, 3)),
+            dma((CHUNKS, 3)),
             pltpu.SemaphoreType.REGULAR((6,)),
             pltpu.SemaphoreType.REGULAR,
         ],
@@ -369,29 +413,30 @@
     )(u, table, xt, ids, stat, h, gain, loss)
 
 
-def table_kernel(emb_ref, norm_ref, h_ref, g_ref, ids_ref, u_ref, table_ref, xt_ref, stat_ref, gain_ref, loss_ref,
-                 xin, mid, yin, tab, norms, norms_in, xn, rhs, ubuf, acc, sums, sums_in,
-                 ex_send, ex_recv, nsend, nrecv, ssem, rsem, psend, precv, usem, tsem):
+def table_kernel(emb_ref, norm_ref, ids_ref, h_hbm, g_hbm, u_ref, table_ref, xt_hbm, stat_ref, gain_ref, loss_ref,
+                 xin, mid, tab, norms, norms_in, xn, rhs, ubuf, acc, sums, sums_in, xt_ref, h_ref, g_ref,
+                 big_sem, ex_send, ex_recv, nsend, nrecv, ssem, rsem, psend, precv, usem, tsem):
     me = lax.axis_index("fsdp")
     tp = lax.axis_index("tp")
     pos = coords(me)
     tokens, width = h_ref.shape
     parts, block, lanes = tab.shape[0], tab.shape[5], tab.shape[6]
-    quarter = emb_ref.shape[2]
+    sub = emb_ref.shape[2]
     cols = emb_ref.shape[1]
-    sub = quarter // 4
+    quarter = NX * sub
     peers = {a: [{"fsdp": shifted(me, pos, a, d)} for d in (1, 2, 3)] for a in "xyz"}
     partner = {"tp": 1 - tp}
-    greet(peers["x"] + peers["y"] + peers["z"] + [partner])
-
-    def exchange(j):
-        axis = "xy"[j]
-        out = []
-        for d in (1, 2, 3):
-            there = lax.rem(pos[axis] + d, 4)
-            src, dst = (emb_ref.at[there], xin.at[pos[axis]]) if j == 0 else (mid.at[there], yin.at[pos[axis]])
-            out.append(remote(src, dst, ex_send.at[j, d - 1], ex_recv.at[j, d - 1], peers[axis][d - 1]))
-        return out
+    plane = NX * NX
+    here = lax.rem(me, plane)
+    field = [{"fsdp": me - here + lax.rem(here + d, plane)} for d in range(1, plane)]
+    big = (pltpu.make_async_copy(h_hbm, h_ref, big_sem.at[0]), pltpu.make_async_copy(g_hbm, g_ref, big_sem.at[1]),
+           pltpu.make_async_copy(xt_ref, xt_hbm, big_sem.at[2]))
+    big[0].start()
+    big[1].start()
+    greet(field + peers["z"] + [partner])
+
+    def exchange():
+        return [remote(emb_ref.at[lax.rem(here + d + 1, plane)], xin.at[here], ex_send.at[d], ex_recv.at[d], n) for d, n in enumerate(field)]
 
     def norm_copies(j):
         return [remote(norms, norms_in.at[j, d], nsend.at[j, d], nrecv.at[j, d], peers["xyz"[j]][d]) for d in range(3)]
@@ -406,28 +451,17 @@
         norms[...] = norms[...] + norms_in[j, 0] + norms_in[j, 1] + norms_in[j, 2]
 
     norms[...] = norm_ref[...]
-    for cp in exchange(0):
+    for cp in exchange():
         cp.start()
-    xin[pos["x"]] = emb_ref[pos["x"]]
     norm_start(0)
-    for cp in exchange(0):
+    xin[here] = emb_ref[here]
+    for cp in exchange():
         cp.wait()
-    for j in range(4):
-        for i in range(4):
-            mid[j, pl.ds(cols * i, cols), :] = xin[i, :, pl.ds(sub * j, sub)]
-    norm_end(0)
-    norm_start(1)
-    for cp in exchange(1):
-        cp.start()
-    yin[pos["y"]] = mid[pos["y"]]
-    for cp in exchange(1):
-        cp.wait()
-    whole = jnp.concatenate([yin[i] for i in range(4)], axis=0).astype(BF16)
+    for i in range(plane):
+        mid[pl.ds(cols * i, cols), :] = xin[i].astype(F32)
     for c in range(parts):
         for k in range(COLORS):
-            tab[c, pos["x"], pos["y"], pos["z"], k] = whole[block * k:block * k + block, lanes * c:lanes * c + lanes]
-    norm_end(1)
-    norm_start(2)
+            tab[c, pos["x"], pos["y"], pos["z"], k] = mid[block * k:block * k + block, lanes * c:lanes * c + lanes].astype(BF16)
 
     def region(e, kind, k, a, half):
         o = ORDERS[k]
@@ -436,12 +470,12 @@
             return tab.at[:, sel["x"], sel["y"], sel["z"], k, pl.ds(half * (block // 2), block // 2)]
         if kind == 1:
             sel = {o[0]: pos[o[0]], o[1]: a, o[2]: pl.ds(2 * half, 2)}
-            return tab.at[:, sel["x"], sel["y"], sel["z"], k]
+            return tab.at[e - 1, sel["x"], sel["y"], sel["z"], k]
         sel = {o[0]: a, o[1]: pl.ds(2 * half, 2), o[2]: slice(None)}
-        return tab.at[e - 2, sel["x"], sel["y"], sel["z"], k]
+        return tab.at[e - 1 - parts, sel["x"], sel["y"], sel["z"], k]
 
     def copies(e, k, step):
-        kind = min(e, 2) if isinstance(e, int) else 2
+        kind = 2 if not isinstance(e, int) or e > parts else min(e, 1)
         axis = ORDERS[k][2 - kind]
         p = pos[axis]
         right, left = lax.rem(p + 1, 4), lax.rem(p + 3, 4)
@@ -474,10 +508,16 @@
             for cp in one + two:
                 cp.wait_send()
 
+    bulk = 1 + parts
+    norm_end(0)
+    norm_start(1)
     begin(0)
+    norm_end(1)
+    norm_start(2)
     forward(0)
     arrive(0)
-    begin(1)
+    for c in range(parts):
+        begin(1 + c)
     norm_end(2)
     n = width // LANE
     gain = 1.0 + jnp.concatenate([norms[pl.ds(i, 1), :] for i in range(n)], axis=1)
@@ -494,11 +534,18 @@
         xt_ref[:, span(tokens + b * LANE, LANE)] = g_ref[r].T
         return carry
 
+    big[0].wait()
+    big[1].wait()
     lax.fori_loop(0, tokens // LANE, normalize, 0)
-    forward(1)
     acc[...] = jnp.zeros_like(acc)
-    arrive(1)
-    begin(2)
+    for c in range(parts):
+        forward(1 + c)
+        if c >= 1:
+            arrive(c)
+            if c <= 2:
+                begin(bulk + c - 1)
+    arrive(parts)
+    forward(bulk)
 
     def u_out(i):
         c, p = lax.div(i, 8), lax.rem(i, 8)
@@ -515,13 +562,11 @@
         return cps
 
     def chunk(c, carry):
-        forward(c + 2)
-
-        @pl.when(c + 1 < parts)
-        def _():
-            begin(c + 3)
-
-        arrive(c + 2)
+        arrive(c + bulk)
+
+        @pl.when(c + 2 < parts)
+        def _():
+            begin(c + 2 + bulk)
 
         @pl.when(c >= 1)
         def _():
@@ -561,14 +606,20 @@
             lax.fori_loop(0, tokens // ROWS, rows, 0, unroll=True)
             for cp in u_out(i):
                 cp.start()
+
+            @pl.when(jnp.logical_and(p == NX - 1, c + 1 < parts))
+            def _():
+                forward(c + 1 + bulk)
             return carry
 
         lax.fori_loop(0, 8, pair, 0)
         return carry
 
+    big[2].start()
     lax.fori_loop(0, parts, chunk, 0)
     lane = lax.broadcasted_iota(jnp.int32, (tokens, LANE), 1)
     sums[...] = jnp.where(lane == 0, jnp.sum(acc[0], axis=1, keepdims=True), jnp.sum(acc[1], axis=1, keepdims=True))
+    big[2].wait()
     swap = remote(sums, sums_in, psend, precv, partner)
     swap.start()
     for cp in u_out(parts * 8 - 2) + u_out(parts * 8 - 1) + table_out(parts - 1):
@@ -582,10 +633,10 @@
 
 def table_pass(emb, norm, h, g, ids):
     tokens, width = h.shape
-    quarter = emb.shape[2]
+    sub = emb.shape[2]
     cols = emb.shape[1]
+    quarter = NX * sub
     vocab = NX * quarter
-    sub = quarter // 4
     block = width // 12
     parts = sub // LANE
     vm = pl.BlockSpec(memory_space=pltpu.VMEM)
@@ -601,12 +652,11 @@
             jax.ShapeDtypeStruct((1, width), F32),
             jax.ShapeDtypeStruct((1, LANE), F32),
         ],
-        in_specs=[vm] * 5,
-        out_specs=[hbm, hbm, vm, vm, vm, vm],
+        in_specs=[vm] * 3 + [hbm] * 2,
+        out_specs=[hbm, hbm, hbm, vm, vm, vm],
         scratch_shapes=[
-            pltpu.VMEM((4, cols, quarter), F32),
-            pltpu.VMEM((4, 4 * cols, sub), F32),
-            pltpu.VMEM((4, 4 * cols, sub), F32),
+            pltpu.VMEM((NX * NX, cols, sub), BF16),
+            pltpu.VMEM((NX * NX * cols, sub), F32),
             pltpu.VMEM((parts, 4, 4, 4, COLORS, block, LANE), BF16),
             pltpu.VMEM((16, LANE), F32),
             pltpu.VMEM((3, 3, 16, LANE), F32),
@@ -616,19 +666,23 @@
             pltpu.VMEM((2, tokens, LANE), F32),
             pltpu.VMEM((tokens, LANE), F32),
             pltpu.VMEM((tokens, LANE), F32),
-            dma((2, 3)),
-            dma((2, 3)),
+            pltpu.VMEM((width, 2 * tokens), BF16),
+            pltpu.VMEM((tokens, width), BF16),
+            pltpu.VMEM((tokens, width), BF16),
+            dma((3,)),
+            dma((NX * NX,)),
+            dma((NX * NX,)),
             dma((3, 3)),
             dma((3, 3)),
-            dma((2 + parts, COLORS, 6)),
-            dma((2 + parts, COLORS, 6)),
+            dma((1 + 2 * parts, COLORS, 6)),
+            dma((1 + 2 * parts, COLORS, 6)),
             dma,
             dma,
             dma((2, 2)),
             dma((4, 4)),
         ],
         compiler_params=pltpu.CompilerParams(collective_id=1, has_side_effects=True, vmem_limit_bytes=63 * 2**20),
-    )(emb, norm, h, g, ids)
+    )(emb, norm, ids, h, g)
     return u, table.reshape(width, vocab), xt, stat, gain, loss
 
 
@@ -639,7 +693,6 @@
 
 def solution(mesh):
     fsdp_size = mesh.shape["fsdp"]
-    x_groups = [[i * NX + j for j in range(NX)] for i in range(fsdp_size // NX)]
 
     def device_step(emb_shard, tok_ids, lab_ids, h_last, g_embed, norm_w):
         vocab_rows, cols = emb_shard.shape
@@ -650,7 +703,7 @@
         row_start = lax.axis_index("tp") * vocab_rows
         me = lax.axis_index("fsdp")
 
-        emb = emb_shard.T.reshape(cols, NX, quarter).transpose(1, 0, 2)
+        emb = emb_shard.T.astype(BF16).reshape(cols, NX, NX, quarter // NX).transpose(2, 1, 0, 3).reshape(NX * NX, cols, quarter // NX)
         norm = lax.dynamic_update_slice(jnp.zeros((16 * LANE,), F32), norm_w, (me * cols,)).reshape(16, LANE)
         ids = jnp.stack([tok_ids.reshape(tok_count) - row_start, lab_ids.reshape(tok_count) - row_start], axis=1)
         h = h_last.reshape(tok_count, width)
@@ -659,8 +712,7 @@
         grad, d_hidden, small, x_emb = gradients(total_tokens, math_scale(width), u, table, xt, ids, stat, h, gain, loss)
         loss_val = small[width // LANE, 0] / total_tokens
         d_norm_w = lax.dynamic_slice(small.reshape(-1), (me * cols,), (cols,))
-        grad = lax.all_to_all(grad.reshape(NX, cols, quarter), "fsdp", split_axis=0, concat_axis=0, axis_index_groups=x_groups)
-        d_table = grad.transpose(1, 0, 2).reshape(cols, vocab_rows).T
+        d_table = grad.T
         return (x_emb.reshape(batch_loc, seq_len, width), loss_val, d_hidden.reshape(batch_loc, seq_len, width), d_norm_w, d_table)
 
     spec_tok = P("fsdp", None)

time: 329 us -> 308 us (0.936)
  waiting for transfers between devices: 7.85 us -> 0 us
  Pallas kernels: 299 us -> 292 us
  local copies, waits for them, and re-layouts: 15 us -> 11.4 us
  starting transfers between devices: 3.49 us -> 0 us
    pallas_call x1, Pallas kernels: 127 us -> 114 us  [table_pass(): pl.pallas_call(table_kernel, out_shape=[jax.ShapeDtypeStruct((tokens, voc...]
    all_to_all x1 -> x0, waiting for transfers between devices: 7.85 us -> none  [device_step(): lax.all_to_all(grad.reshape(NX, cols, quarter), 'fsdp', split_axis=0, con...]
    pallas_call x1, Pallas kernels: 172 us -> 179 us  [gradients(): pl.pallas_call(functools.partial(grad_kernel, total_tokens, emb_scale), o...]
    reshape x3 -> x2, local copies, waits for them, and re-layouts: 4.77 us -> 1.09 us  [device_step(): emb_shard.T.astype(BF16).reshape(cols, NX, NX, quarter // NX)]
    all_to_all x1 -> x0, starting transfers between devices: 3.49 us -> none  [device_step(): lax.all_to_all(grad.reshape(NX, cols, quarter), 'fsdp', split_axis=0, con...]
  transfers between devices with their start and end apart: 1 -> 0, of which waited for: 1 -> 0; matrix products, arithmetic and copies ran while one was open for 1% -> 0% of each run, Pallas kernels for 0% -> 0%
where the time goes in v4:
time: 308 us
  Pallas kernels  292 us (95%)
  local copies, waits for them, and re-layouts  11.4 us (4%)
    pallas_call x1, Pallas kernels, gradients(): pl.pallas_call(functools.partial(grad_kernel, total_tokens, emb_scale), o...  179 us
    pallas_call x1, Pallas kernels, table_pass(): pl.pallas_call(table_kernel, out_shape=[jax.ShapeDtypeStruct((tokens, voc...  114 us

profile of v4, /device:TPU:0, one launch (start us, length us, event | category | flops | bytes accessed | tf_op | source)
XLA Modules:
  0.0 308.0 jit_solution(9265753840280014180)
XLA Ops:
  0.6 0.7 subtract_bitcast_fusion
  1.4 0.9 dynamic_update_slice.3
  2.2 0.0 copy-start.2
  2.2 1.2 convert_bitcast_fusion
  3.4 0.2 reshape.65
  3.6 0.9 copy.15
  4.5 1.0 copy.16.ids_ref
  5.5 0.0 copy-done.2
  5.6 113.5 %shard_map.101 = (f32[1024,8192]{1,0:T(8,128)}, bf16[4,3,96,8192]{3,2,1,0:T(8,128)(2,1)}, bf16[1152,2048]{1,0:T(8,128)(2,1)}, f32[1024,2]{1,0:T(8,128)}, f32[1,1152]{1,0:T(1,128)}, /*index=5*/f32[1,128]{1,0:T(1,128)}) custom-call(bf16[16,18,512]{2,1,0:T(8,128)(2,1)} %bitcast.24, f32[16,128]{1,0:T(8,128)} %bitcast.26, s32[1024,2]{1,0:T(8,128)} %copy.16.ids_ref, ...), custom_call_target="tpu_custom_call" | custom-call | tf_op jit(solution)/shard_map/pallas_call | solution.py:645
  119.1 178.7 %shard_map.102 = (f32[18,8192]{1,0:T(8,128)}, bf16[1024,1152]{1,0:T(8,128)(2,1)}, f32[16,128]{1,0:T(8,128)}, bf16[1024,1152]{1,0:T(8,128)(2,1)}) custom-call(f32[1024,8192]{1,0:T(8,128)} %get-tuple-element.15.u_ref, bf16[1152,8192]{1,0:T(8,128)(2,1)} %bitcast.18, bf16[1152,2048]{1,0:T(8,128)(2,1)} %get-tuple-element.17.xt_ref, s32[1024,2]{1,0:T(8,128)} %copy.16.ids_ref, ...), custom_call_target="tpu_custom_call" | custom-call | tf_op jit(solution)/shard_map/pallas_call | solution.py:377
  297.7 1.2 slice.3
  299.6 1.3 dynamic_slice.3
  300.9 0.0 copy-start
  300.9 3.4 %copy.22 = bf16[1,1024,1152]{2,1,0:T(8,128)(2,1)} copy(bf16[1,1024,1152]{2,1,0:T(8,128)(2,1)} %bitcast.23) | data formatting | bytes 4718592
  304.3 0.0 copy-done
  304.3 0.0 copy-start.1
  304.3 1.4 copy.23
  305.7 0.3 copy-done.1
  306.0 0.9 copy.24
  (2 shorter events, 0.0 us)
Async XLA Ops:
  2.2 3.3 %copy-start.2 = (f32[2048]{0:T(1024)}, f32[2048]{0:T(1024)S(1)}, u32[]{:S(2)}) copy-start(f32[2048]{0:T(1024)S(1)} %dynamic_update_slice.3) | copy-start | bytes 24580
  300.9 3.4 %copy-start = (bf16[1024,1152]{1,0:T(8,128)(2,1)S(1)}, bf16[1024,1152]{1,0:T(8,128)(2,1)}, u32[]{:S(2)}) copy-start(bf16[1024,1152]{1,0:T(8,128)(2,1)} %get-tuple-element.23) | copy-start | bytes 7077892
  304.3 1.7 copy-start.1

commit v5 on v4

--- a/solution.py
+++ b/solution.py
@@ -287,10 +287,10 @@
         else:
             sums[...] = sums[...] + sums_in[phase, 0] + sums_in[phase, 1] + sums_in[phase, 2]
 
+    for cp in loads(0):
+        cp.start()
     dxn[...] = jnp.zeros_like(dxn)
     look_ref[...] = jnp.zeros_like(look_ref)
-    for cp in loads(0):
-        cp.start()
     ticks = chunks + 7
 
     def tick(t, carry):
@@ -321,6 +321,7 @@
             last(1, c, store2(lax.rem(c, SLOTS)))
             first(2, c)
 
+        stage(1, lambda c: second(0, c))
         stage(0, lambda c: first(0, c))
         @pl.when(t == chunks - 1)
         def _():
@@ -332,7 +333,6 @@
         stage(4, s4)
         stage(3, lambda c: second(1, c))
         stage(2, s2)
-        stage(1, lambda c: second(0, c))
 
         @pl.when(t == chunks)
         def _():

time: 308 us -> 307 us (level)
  no operation moved by 1% of the time
where the time goes in v5:
time: 307 us
  Pallas kernels  291 us (95%)
  local copies, waits for them, and re-layouts  11.4 us (4%)
    pallas_call x1, Pallas kernels, gradients(): pl.pallas_call(functools.partial(grad_kernel, total_tokens, emb_scale), o...  178 us
    pallas_call x1, Pallas kernels, table_pass(): pl.pallas_call(table_kernel, out_shape=[jax.ShapeDtypeStruct((tokens, voc...  114 us

profile of v5, /device:TPU:0, one launch (start us, length us, event | category | flops | bytes accessed | tf_op | source)
XLA Modules:
  0.0 306.8 jit_solution(2133593316548434046)
XLA Ops:
  0.6 0.7 subtract_bitcast_fusion
  1.4 0.9 dynamic_update_slice.3
  2.2 0.0 copy-start.2
  2.2 1.2 convert_bitcast_fusion
  3.4 0.2 reshape.65
  3.6 0.9 copy.15
  4.5 1.0 copy.16.ids_ref
  5.5 0.0 copy-done.2
  5.6 113.5 %shard_map.101 = (f32[1024,8192]{1,0:T(8,128)}, bf16[4,3,96,8192]{3,2,1,0:T(8,128)(2,1)}, bf16[1152,2048]{1,0:T(8,128)(2,1)}, f32[1024,2]{1,0:T(8,128)}, f32[1,1152]{1,0:T(1,128)}, /*index=5*/f32[1,128]{1,0:T(1,128)}) custom-call(bf16[16,18,512]{2,1,0:T(8,128)(2,1)} %bitcast.24, f32[16,128]{1,0:T(8,128)} %bitcast.26, s32[1024,2]{1,0:T(8,128)} %copy.16.ids_ref, ...), custom_call_target="tpu_custom_call" | custom-call | tf_op jit(solution)/shard_map/pallas_call | solution.py:645
  119.1 177.5 %shard_map.102 = (f32[18,8192]{1,0:T(8,128)}, bf16[1024,1152]{1,0:T(8,128)(2,1)}, f32[16,128]{1,0:T(8,128)}, bf16[1024,1152]{1,0:T(8,128)(2,1)}) custom-call(f32[1024,8192]{1,0:T(8,128)} %get-tuple-element.15.u_ref, bf16[1152,8192]{1,0:T(8,128)(2,1)} %bitcast.18, bf16[1152,2048]{1,0:T(8,128)(2,1)} %get-tuple-element.17.xt_ref, s32[1024,2]{1,0:T(8,128)} %copy.16.ids_ref, ...), custom_call_target="tpu_custom_call" | custom-call | tf_op jit(solution)/shard_map/pallas_call | solution.py:377
  296.6 1.2 slice.3
  298.4 1.3 dynamic_slice.3
  299.7 0.0 copy-start
  299.7 3.4 %copy.22 = bf16[1,1024,1152]{2,1,0:T(8,128)(2,1)} copy(bf16[1,1024,1152]{2,1,0:T(8,128)(2,1)} %bitcast.23) | data formatting | bytes 4718592
  303.1 0.0 copy-done
  303.1 0.0 copy-start.1
  303.1 1.4 copy.23
  304.5 0.3 copy-done.1
  304.8 0.9 copy.24
  (2 shorter events, 0.0 us)
Async XLA Ops:
  2.2 3.3 %copy-start.2 = (f32[2048]{0:T(1024)}, f32[2048]{0:T(1024)S(1)}, u32[]{:S(2)}) copy-start(f32[2048]{0:T(1024)S(1)} %dynamic_update_slice.3) | copy-start | bytes 24580
  299.7 3.4 %copy-start = (bf16[1024,1152]{1,0:T(8,128)(2,1)S(1)}, bf16[1024,1152]{1,0:T(8,128)(2,1)}, u32[]{:S(2)}) copy-start(bf16[1024,1152]{1,0:T(8,128)(2,1)} %get-tuple-element.23) | copy-start | bytes 7077892
  303.1 1.7 copy-start.1
